TPU v7x, 64 devices: a 2x2x8 block of a 4x4x8 slice. The times are simulated.
64 devices in a mesh: stage: 4 (over x, y), data: 16 (over z, core).
Axes of the slice: x: 2, y: 2, z: 8, core: 2. Of those that a mesh axis runs over, the one named last changes fastest.
The devices are a block of a 4x4x8 slice.
Arguments:
- grad_attn: float32 [64, 1, 1536, 1536], P(('stage', 'data')), parts along dimension 0
- mom_attn: float32 [4, 1536, 1536], P('stage', 'data'), parts along dimension 0
- master_attn: float32 [4, 1536, 1536], P('stage', 'data'), parts along dimension 0
- grad_up: float32 [64, 1, 1536, 512], P(('stage', 'data')), parts along dimension 0
- mom_up: float32 [4, 1536, 512], P('stage', 'data'), parts along dimension 0
- master_up: float32 [4, 1536, 512], P('stage', 'data'), parts along dimension 0
- grad_down: float32 [64, 1, 512, 1536], P(('stage', 'data')), parts along dimension 0
- mom_down: float32 [4, 512, 1536], P('stage', 'data'), parts along dimension 0
- master_down: float32 [4, 512, 1536], P('stage', 'data'), parts along dimension 0
Outputs:
- output 1: float32 [4, 1536, 1536], P('stage', 'data'), parts along dimension 0
- output 2: float32 [4, 1536, 1536], P('stage', 'data'), parts along dimension 0
- output 3: bfloat16 [4, 1536, 1536], P('stage', 'data'), parts along dimension 0
- output 4: float32 [4, 1536, 512], P('stage', 'data'), parts along dimension 0
- output 5: float32 [4, 1536, 512], P('stage', 'data'), parts along dimension 0
- output 6: bfloat16 [4, 1536, 512], P('stage', 'data'), parts along dimension 0
- output 7: float32 [4, 512, 1536], P('stage', 'data'), parts along dimension 0
- output 8: float32 [4, 512, 1536], P('stage', 'data'), parts along dimension 0
- output 9: bfloat16 [4, 512, 1536], P('stage', 'data'), parts along dimension 0
There are 4 independent parts. A program takes and returns all parts, laid end to end along the dimension named above; each array names one.
All inputs are finite; a program needn't handle non-finite values.
Results may differ from a plain program's by a relative error of at most 0.00769194.
Values are sent between devices in bfloat16 or wider.
A program may use at most 768 MiB of HBM per device.

v0:
```python
import math
import functools
import jax
import jax.numpy as jnp
from jax import lax
from jax.sharding import PartitionSpec as P, NamedSharding

MOMENTUM = 0.95
LEARN_RATE = 0.25
WEIGHT_DECAY = 0.2
EPSILON = 1e-7
COEF_A = 3.4445
COEF_B = -4.7750
COEF_C = 2.0315
NS_STEPS = 5


def newton_schulz(x_mat, is_tall):
    for _ in range(NS_STEPS):
        if is_tall:
            gram_mat = jnp.einsum('bkr,bkc->brc', x_mat, x_mat, preferred_element_type=jnp.float32)
        else:
            gram_mat = jnp.einsum('brk,bck->brc', x_mat, x_mat, preferred_element_type=jnp.float32)
        gram_mat = gram_mat.astype(jnp.bfloat16)
        gram_sq = jnp.einsum('brk,bkc->brc', gram_mat, gram_mat, preferred_element_type=jnp.float32).astype(jnp.bfloat16)
        poly_mat = (COEF_B * gram_mat.astype(jnp.float32) + COEF_C * gram_sq.astype(jnp.float32)).astype(jnp.bfloat16)
        if is_tall:
            update = jnp.einsum('bkc,brc->bkr', x_mat, poly_mat, preferred_element_type=jnp.float32)
        else:
            update = jnp.einsum('brc,bck->brk', poly_mat, x_mat, preferred_element_type=jnp.float32)
        x_mat = (COEF_A * x_mat.astype(jnp.float32) + update.astype(jnp.bfloat16).astype(jnp.float32)).astype(jnp.bfloat16)
    return x_mat


def stack_step(grad_all, mom_old, master_old, offset, group_size):
    count, rows_local, n_cols = mom_old.shape
    n_rows = rows_local * group_size
    grad_rows = lax.psum_scatter(grad_all[0], 'data', scatter_dimension=1, tiled=True) / group_size
    mom_new = MOMENTUM * mom_old + grad_rows
    norm_sq = lax.psum(jnp.sum(mom_new * mom_new, axis=(1, 2)), 'data')
    x_rows = (mom_new / (jnp.sqrt(norm_sq)[:, None, None] + EPSILON)).astype(jnp.bfloat16)
    slots = (count + offset + group_size - 1) // group_size
    padded = jnp.pad(x_rows, ((offset, slots * group_size - count - offset), (0, 0), (0, 0)))
    send_buf = padded.reshape(slots, group_size, rows_local, n_cols)
    owned = lax.all_to_all(send_buf, 'data', 1, 2, tiled=True).reshape(slots, n_rows, n_cols)
    positions = jnp.arange(slots) * group_size + lax.axis_index('data')
    has_work = jnp.any((positions >= offset) & (positions < offset + count))
    ortho_mat = lax.cond(has_work, functools.partial(newton_schulz, is_tall=n_rows > n_cols), jnp.zeros_like, owned)
    returned = lax.all_to_all(ortho_mat.reshape(slots, 1, n_rows, n_cols), 'data', 2, 1, tiled=True)
    ortho_rows = returned.reshape(slots * group_size, rows_local, n_cols)[offset:offset + count]
    scale = 0.2 * math.sqrt(max(n_rows, n_cols))
    master_new = master_old - LEARN_RATE * (scale * ortho_rows.astype(jnp.float32) + WEIGHT_DECAY * master_old)
    return [mom_new, master_new, master_new.astype(jnp.bfloat16)]


def solution(mesh):
    group_size = mesh.shape['data']
    grad_spec = P(('stage', 'data'), None, None, None)
    row_spec = P('stage', 'data', None)

    def step_local(*arrays):
        attn_count = arrays[1].shape[0]
        expert_count = arrays[4].shape[0]
        offsets = (0, attn_count % group_size, (attn_count + expert_count) % group_size)
        results = []
        for stack_idx in range(3):
            results.extend(stack_step(arrays[3 * stack_idx], arrays[3 * stack_idx + 1], arrays[3 * stack_idx + 2], offsets[stack_idx], group_size))
        return tuple(results)

    in_specs = (grad_spec, row_spec, row_spec) * 3
    out_specs = (row_spec,) * 9
    return jax.shard_map(step_local, mesh=mesh, in_specs=in_specs, out_specs=out_specs, check_vma=False)
```

profile of v0, /device:TPU:21, one launch (start us, length us, event | category | flops | bytes accessed | tf_op | source)
XLA Modules:
  0.0 866.0 jit_solution(15067851882233763083)
XLA Ops:
  9.6 60.8 %reduce-scatter.6.cloned.1.call-done = f32[1,96,512]{2,1,0:T(8,128)} async-done(((f32[1,1536,512]{2,1,0:T(8,128)}), f32[1,96,512]{2,1,0:T(8,128)}) %reduce-scatter.6.cloned.1.call-update) | async-done | bytes 196624 | tf_op jit(solution)/shard_map/reduce_scatter | solution.py:38
  72.0 57.7 %reduce-scatter.8.cloned.1.call-done = f32[1,32,1536]{2,1,0:T(8,128)} async-done(((f32[1,512,1536]{2,1,0:T(8,128)}), f32[1,32,1536]{2,1,0:T(8,128)}) %reduce-scatter.8.cloned.1.call-update) | async-done | bytes 196624 | tf_op jit(solution)/shard_map/reduce_scatter | solution.py:38
  131.3 69.2 %reduce-scatter.4.cloned.1.call-done = f32[1,96,1536]{2,1,0:T(8,128)} async-done(((f32[1,1536,1536]{2,1,0:T(8,128)}), f32[1,96,1536]{2,1,0:T(8,128)}) %reduce-scatter.4.cloned.1.call-update) | async-done | bytes 589840 | tf_op jit(solution)/shard_map/reduce_scatter | solution.py:38
  203.0 26.9 %all-reduce.3 = (f32[1]{0:T(128)}, f32[1]{0:T(128)}, f32[1]{0:T(128)}) all-reduce(f32[1]{0:T(128)} %bitcast.16, f32[1]{0:T(128)} %bitcast.22, f32[1]{0:T(128)} %bitcast.28), channel_id=1, replica_groups=mesh['stage'=4,'data'=16] {'data'}, use_global_device_ids=true, to_apply=%region_2.0 | all-reduce | flops 3 | bytes 24 | tf_op jit(solution)/shard_map/psum | solution.py:40
  231.9 7.7 all-to-all-start.4
  241.7 36.3 %all-to-all-done.4 = bf16[1,16,32,1536]{3,2,0,1:T(8,128)(2,1)S(1)} async-done(((bf16[1,16,32,1536]{3,2,0,1:T(8,128)(2,1)}), bf16[1,16,32,1536]{3,2,0,1:T(8,128)(2,1)S(1)}, u32[]{:S(2)}, u32[]{:S(2)}) %all-to-all-start.4) | async-done | bytes 1572896 | tf_op jit(solution)/shard_map/all_to_all | solution.py:45
  288.3 11.6 %reduce.5 = bf16[512,1536]{1,0:T(8,128)(2,1)} reduce(bf16[512,1,1,1536]{3,2,1,0:T(2,128)(2,1)S(1)} %bitcast.203, bf16[]{:T(256)} %broadcast.268), dimensions={1,2}, to_apply=%bitcast.199.reduce_sub_computation | reduce | bytes 3145730
  304.9 15.6 %all-to-all-done.2 = bf16[1,16,96,512]{3,2,0,1:T(8,128)(2,1)} async-done(((bf16[1,16,96,512]{3,2,0,1:T(8,128)(2,1)}), bf16[1,16,96,512]{3,2,0,1:T(8,128)(2,1)}, u32[]{:S(2)}, u32[]{:S(2)}) %all-to-all-start.2) | async-done | bytes 1572896 | tf_op jit(solution)/shard_map/all_to_all | solution.py:45
  320.5 11.5 %all-to-all-start.5 = ((bf16[16,2,24576]{2,1,0:T(2,128)(2,1)}), bf16[16,2,24576]{2,1,0:T(2,128)(2,1)S(1)}, u32[]{:S(2)}, u32[]{:S(2)}) async-start(bf16[16,2,24576]{2,1,0:T(2,128)(2,1)} %reshape.606), calls=%async_computation.8 | async-start | bytes 3145728 | tf_op jit(solution)/shard_map/all_to_all | solution.py:49
  335.4 34.7 %all-to-all-done.5 = bf16[16,2,24576]{2,1,0:T(2,128)(2,1)S(1)} async-done(((bf16[16,2,24576]{2,1,0:T(2,128)(2,1)}), bf16[16,2,24576]{2,1,0:T(2,128)(2,1)S(1)}, u32[]{:S(2)}, u32[]{:S(2)}) %all-to-all-start.5) | async-done | bytes 1572896 | tf_op jit(solution)/shard_map/all_to_all | solution.py:49
  376.0 29.1 %conditional.4 = (bf16[1,1536,512]{1,2,0:T(8,128)(2,1)S(1)}) conditional(s32[]{:T(128)} %convert_element_type.629, () %tuple.27, bf16[1,16,96,512]{3,2,0,1:T(8,128)(2,1)} %all-to-all-done.2), branch_computations={%region_8.9_spmd, %region_9.10_spmd} | conditional | flops 9429319680 | bytes 39845924 | solution.py:48
  406.3 6.8 copy.48
  413.1 11.1 %reduce.4 = bf16[1536,512]{1,0:T(8,128)(2,1)} reduce(bf16[1536,1,1,512]{3,2,1,0:T(2,128)(2,1)S(1)} %bitcast.204, bf16[]{:T(256)} %broadcast.268), dimensions={1,2}, to_apply=%bitcast.71.reduce_sub_computation | reduce | bytes 3145730
  429.2 51.9 %all-to-all-done = bf16[1,16,96,1536]{3,2,0,1:T(8,128)(2,1)} async-done(((bf16[1,16,96,1536]{3,2,0,1:T(8,128)(2,1)}), bf16[1,16,96,1536]{3,2,0,1:T(8,128)(2,1)}, u32[]{:S(2)}, u32[]{:S(2)}) %all-to-all-start) | async-done | bytes 4718624 | tf_op jit(solution)/shard_map/all_to_all | solution.py:45
  481.1 9.1 %all-to-all-start.3 = ((bf16[16,2,24576]{2,1,0:T(2,128)(2,1)}), bf16[16,2,24576]{2,1,0:T(2,128)(2,1)}, u32[]{:S(2)}, u32[]{:S(2)}) async-start(bf16[16,2,24576]{2,1,0:T(2,128)(2,1)} %reshape.604), calls=%async_computation.5 | async-start | bytes 3145728 | tf_op jit(solution)/shard_map/all_to_all | solution.py:49
  490.2 7.8 conditional.3
  498.0 9.6 %copy.62 = bf16[1,1,1536,1536]{3,1,0,2:T(2,128)(2,1)} copy(bf16[1,1,1536,1536]{3,2,1,0:T(8,128)(2,1)} %bitcast.202) | data formatting | bytes 9437184 | tf_op jit(solution)/shard_map/reshape | solution.py:49
  507.6 32.0 %reduce.3 = bf16[1536,1536]{1,0:T(8,128)(2,1)} reduce(bf16[1536,1,1,1536]{3,2,1,0:T(2,128)(2,1)} %bitcast.200, bf16[]{:T(256)} %broadcast.268), dimensions={1,2}, to_apply=%bitcast.198.reduce_sub_computation | reduce | bytes 9437186
  539.6 11.8 %reshape.602 = bf16[16,2,73728]{2,1,0:T(2,128)(2,1)} reshape(bf16[1536,1536]{1,0:T(8,128)(2,1)} %reduce.3) | data formatting | bytes 9437184
  551.4 184.3 %all-to-all-start.1 = ((bf16[16,2,73728]{2,1,0:T(2,128)(2,1)}), bf16[16,2,73728]{2,1,0:T(2,128)(2,1)}, u32[]{:S(2)}, u32[]{:S(2)}) async-start(bf16[16,2,73728]{2,1,0:T(2,128)(2,1)} %reshape.602), calls=%async_computation.2 | async-start | bytes 9437184 | tf_op jit(solution)/shard_map/all_to_all | solution.py:49
  735.6 8.1 reshape.607
  745.3 8.1 reshape.605
  756.3 84.0 %all-to-all-done.1 = bf16[16,2,73728]{2,1,0:T(2,128)(2,1)} async-done(((bf16[16,2,73728]{2,1,0:T(2,128)(2,1)}), bf16[16,2,73728]{2,1,0:T(2,128)(2,1)}, u32[]{:S(2)}, u32[]{:S(2)}) %all-to-all-start.1) | async-done | bytes 4718624 | tf_op jit(solution)/shard_map/all_to_all | solution.py:49
  840.3 12.8 %reshape.603 = bf16[1536,1,1,1536]{3,2,1,0:T(2,128)(2,1)} reshape(bf16[16,2,73728]{2,1,0:T(2,128)(2,1)} %all-to-all-done.1) | data formatting | bytes 9437184
  (68 shorter events, 82.3 us)
Async XLA Ops:
  7.2 63.2 %reduce-scatter.6.cloned.1.call-start = ((), (), s32[]{:S(2)}) async-start(), calls=%async_computation.10 | async-start | bytes 3342336 | tf_op jit(solution)/shard_map/reduce_scatter | solution.py:38
  8.0 121.7 %reduce-scatter.8.cloned.1.call-start = ((), (), s32[]{:S(2)}) async-start(), calls=%async_computation.11 | async-start | bytes 3342336 | tf_op jit(solution)/shard_map/reduce_scatter | solution.py:38
  8.8 191.6 %reduce-scatter.4.cloned.1.call-start = ((), (), s32[]{:S(2)}) async-start(), calls=%async_computation.9 | async-start | bytes 10027008 | tf_op jit(solution)/shard_map/reduce_scatter | solution.py:38
  8.9 61.5 %copy-start.8 = (f32[1,96,512]{2,1,0:T(8,128)S(1)}, f32[1,96,512]{2,1,0:T(8,128)}, u32[]{:S(2)}) copy-start(f32[1,96,512]{2,1,0:T(8,128)} %param.19) | copy-start | bytes 589828
  8.9 120.8 %copy-start.9 = (f32[1,32,1536]{2,1,0:T(8,128)S(1)}, f32[1,32,1536]{2,1,0:T(8,128)}, u32[]{:S(2)}) copy-start(f32[1,32,1536]{2,1,0:T(8,128)} %param.22) | copy-start | bytes 589828
  8.9 191.5 %copy-start.7 = (f32[1,96,1536]{2,1,0:T(8,128)S(1)}, f32[1,96,1536]{2,1,0:T(8,128)}, u32[]{:S(2)}) copy-start(f32[1,96,1536]{2,1,0:T(8,128)} %param.16) | copy-start | bytes 1769476
  72.0 169.7 %copy-start.4 = (f32[1,96,512]{2,1,0:T(8,128)}, f32[1,96,512]{2,1,0:T(8,128)S(1)}, u32[]{:S(2)}) copy-start(f32[1,96,512]{2,1,0:T(8,128)S(1)} %get-tuple-element.36) | copy-start | bytes 589828
  131.3 146.7 %copy-start.5 = (f32[1,32,1536]{2,1,0:T(8,128)}, f32[1,32,1536]{2,1,0:T(8,128)S(1)}, u32[]{:S(2)}) copy-start(f32[1,32,1536]{2,1,0:T(8,128)S(1)} %get-tuple-element.34) | copy-start | bytes 589828
  231.9 46.0 %all-to-all-start.4 = ((bf16[1,16,32,1536]{3,2,0,1:T(8,128)(2,1)}), bf16[1,16,32,1536]{3,2,0,1:T(8,128)(2,1)S(1)}, u32[]{:S(2)}, u32[]{:S(2)}) async-start(bf16[1,16,32,1536]{3,2,0,1:T(8,128)(2,1)} %pad_bitcast_fusion.1), calls=%async_computation.7 | async-start | bytes 3145728 | tf_op jit(solution)/shard_map/all_to_all | solution.py:45
  277.9 42.6 %all-to-all-start.2 = ((bf16[1,16,96,512]{3,2,0,1:T(8,128)(2,1)}), bf16[1,16,96,512]{3,2,0,1:T(8,128)(2,1)}, u32[]{:S(2)}, u32[]{:S(2)}) async-start(bf16[1,16,96,512]{3,2,0,1:T(8,128)(2,1)} %pad_bitcast_fusion.2), calls=%async_computation.4 | async-start | bytes 3145728 | tf_op jit(solution)/shard_map/all_to_all | solution.py:45
  282.8 1.1 copy-start.1
  299.9 32.8 %copy-start.3 = (f32[1,96,1536]{2,1,0:T(8,128)S(1)}, f32[1,96,1536]{2,1,0:T(8,128)}, u32[]{:S(2)}) copy-start(f32[1,96,1536]{2,1,0:T(8,128)} %get-tuple-element.38) | copy-start | bytes 1769476
  320.5 49.6 %all-to-all-start.5 = ((bf16[16,2,24576]{2,1,0:T(2,128)(2,1)}), bf16[16,2,24576]{2,1,0:T(2,128)(2,1)S(1)}, u32[]{:S(2)}, u32[]{:S(2)}) async-start(bf16[16,2,24576]{2,1,0:T(2,128)(2,1)} %reshape.606), calls=%async_computation.8 | async-start | bytes 3145728 | tf_op jit(solution)/shard_map/all_to_all | solution.py:49
  370.1 1.2 copy-start
  371.3 109.7 %all-to-all-start = ((bf16[1,16,96,1536]{3,2,0,1:T(8,128)(2,1)}), bf16[1,16,96,1536]{3,2,0,1:T(8,128)(2,1)}, u32[]{:S(2)}, u32[]{:S(2)}) async-start(bf16[1,16,96,1536]{3,2,0,1:T(8,128)(2,1)} %pad_bitcast_fusion), calls=%async_computation.1 | async-start | bytes 9437184 | tf_op jit(solution)/shard_map/all_to_all | solution.py:45
  384.5 3.9 copy-start.13
  405.1 1.1 copy-start.2
  481.1 70.3 %all-to-all-start.3 = ((bf16[16,2,24576]{2,1,0:T(2,128)(2,1)}), bf16[16,2,24576]{2,1,0:T(2,128)(2,1)}, u32[]{:S(2)}, u32[]{:S(2)}) async-start(bf16[16,2,24576]{2,1,0:T(2,128)(2,1)} %reshape.604), calls=%async_computation.5 | async-start | bytes 3145728 | tf_op jit(solution)/shard_map/all_to_all | solution.py:49
  551.4 288.9 %all-to-all-start.1 = ((bf16[16,2,73728]{2,1,0:T(2,128)(2,1)}), bf16[16,2,73728]{2,1,0:T(2,128)(2,1)}, u32[]{:S(2)}, u32[]{:S(2)}) async-start(bf16[16,2,73728]{2,1,0:T(2,128)(2,1)} %reshape.602), calls=%async_computation.2 | async-start | bytes 9437184 | tf_op jit(solution)/shard_map/all_to_all | solution.py:49
  745.3 8.6 copy-start.10
  745.3 9.4 %copy-start.11 = (f32[1,32,1536]{2,1,0:T(8,128)S(1)}, f32[1,32,1536]{2,1,0:T(8,128)}, u32[]{:S(2)}) copy-start(f32[1,32,1536]{2,1,0:T(8,128)} %param.23) | copy-start | bytes 589828
  853.1 5.1 copy-start.6
Sparse Core Ops, SparseCore 0:
  10.4 59.9 reduce-scatter.5
  72.7 56.8 reduce-scatter.7
  132.0 68.3 reduce-scatter.3
where the time goes:
time: 876 us; the launch traced here: 866 us
  waiting for transfers between devices  412 us (47%)
  starting transfers between devices  222 us (25%)
  local copies, waits for them, and re-layouts  91.6 us (10%)
  other arithmetic  63.9 us (7%)
  blocking collectives  26.9 us (3%)
  matrix products  26.9 us (3%)
  between operations  16.3 us (2%)
    all_to_all x3, starting transfers between devices, stack_step(): lax.all_to_all(ortho_mat.reshape(slots, 1, n_rows, n_cols), 'data', 2, 1,...  205 us
    reduce_scatter x3, waiting for transfers between devices, stack_step(): lax.psum_scatter(grad_all[0], 'data', scatter_dimension=1, tiled=True)  188 us
    all_to_all x3, waiting for transfers between devices, stack_step(): lax.all_to_all(ortho_mat.reshape(slots, 1, n_rows, n_cols), 'data', 2, 1,...  119 us
    all_to_all x3, waiting for transfers between devices, stack_step(): lax.all_to_all(send_buf, 'data', 1, 2, tiled=True)  104 us
    unnamed x34, local copies, waits for them, and re-layouts  61.8 us
    unnamed x3, other arithmetic  54.7 us
    psum x1, blocking collectives, stack_step(): norm_sq = lax.psum(jnp.sum(mom_new * mom_new, axis=(1, 2)), 'data')  26.9 us
    reshape x3, local copies, waits for them, and re-layouts, stack_step(): ortho_mat.reshape(slots, 1, n_rows, n_cols)  20.3 us
  transfers between devices with their start and end apart: 9, of which 8 were waited for; matrix products, arithmetic and copies ran while one was open for 18% of the time, Pallas kernels for 0%

commit v1 on v0

v1 whole, which is shorter than its diff:
```python
import functools
import math
import jax
import jax.numpy as jnp
from jax import lax
from jax.experimental import pallas as pl
from jax.experimental.pallas import tpu as pltpu
from jax.sharding import PartitionSpec as P

MOMENTUM = 0.95
LEARN_RATE = 0.25
WEIGHT_DECAY = 0.2
EPSILON = 1e-7
COEF_A = 3.4445
COEF_B = -4.7750
COEF_C = 2.0315
NS_STEPS = 5
F32 = jnp.float32
BF16 = jnp.bfloat16


def dot_nn(a, b):
    return lax.dot_general(a, b, (((1,), (0,)), ((), ())), preferred_element_type=F32)


def dot_nt(a, b):
    return lax.dot_general(a, b, (((1,), (1,)), ((), ())), preferred_element_type=F32)


def remote(src, dst, send_sem, recv_sem, dev):
    return pltpu.make_async_remote_copy(
        src_ref=src, dst_ref=dst, send_sem=send_sem, recv_sem=recv_sem,
        device_id={'data': dev}, device_id_type=pl.DeviceIdType.MESH)


def ds(start, size, mult):
    return pl.ds(pl.multiple_of(start, mult), size)


class Place:
    def __init__(self, group):
        self.group = group
        self.chips = group // 2
        self.me = lax.axis_index('data')
        self.chip = self.me // 2
        self.core = self.me % 2
        self.partner = self.chip * 2 + (1 - self.core)

    def at(self, offset):
        return lax.rem(self.chip + offset + self.chips, self.chips)

    def next(self, way):
        return self.at(1 if way == 0 else -1) * 2 + self.core


class Scatter:
    def __init__(self, place, grad, own, pair, ring, load, psend, precv, rsend, rrecv):
        self.pl, self.grad, self.own, self.pair, self.ring = place, grad, own, pair, ring
        self.load, self.psend, self.precv, self.rsend, self.rrecv = load, psend, precv, rsend, rrecv
        self.rows = own.shape[1]
        self.half_rows = self.rows // 2
        self.n = place.chips
        self.pieces = self.n - 1

    def order(self):
        far = self.n // 2
        order = [far]
        for d in range(far - 1, 0, -1):
            order += [d, self.n - d]
        return order + [0]

    def load_copy(self, d):
        row = (self.pl.at(d) * 2 + self.pl.core) * self.rows
        return pltpu.make_async_copy(self.grad.at[ds(row, self.rows, 32), :], self.own.at[d], self.load.at[d])

    def pair_copy(self, d):
        row = (self.pl.at(d) * 2 + (1 - self.pl.core)) * self.rows
        return remote(self.grad.at[ds(row, self.rows, 32), :], self.pair.at[d], self.psend.at[d], self.precv.at[d], self.pl.partner)

    def start(self):
        for d in self.order():
            self.pair_copy(d).start()
            self.load_copy(d).start()

    def arrive(self, d):
        self.load_copy(d).wait()
        self.pair_copy(d).wait_recv()

    def spot(self, way, q):
        dist = self.n // 2 - (q + 1) // 2
        half = way if q % 2 == 0 else 1 - way
        return dist, (dist if way == 0 else (self.n - dist) % self.n), pl.ds(half * self.half_rows, self.half_rows)

    def ring_copy(self, way, q):
        dist, d, rows = self.spot(way, q)
        return remote(self.own.at[d, rows, :], self.ring.at[way, dist - 1, rows, :], self.rsend.at[way, q], self.rrecv.at[way, q], self.pl.next(way))

    def step(self, q):
        for way in (0, 1):
            dist, d, rows = self.spot(way, q)
            if q % 2 == 1 or (q == 0 and way == 0):
                self.arrive(d)
            total = self.own[d, rows, :] + self.pair[d, rows, :]
            if q >= 2:
                self.ring_copy(way, q - 2).wait_recv()
                total = total + self.ring[way, dist, rows, :]
            self.own[d, rows, :] = total
            self.ring_copy(way, q).start()

    def total(self):
        self.arrive(0)
        for way in (0, 1):
            for q in (self.pieces - 2, self.pieces - 1):
                self.ring_copy(way, q).wait_recv()
        return (self.own[0] + self.pair[0]) + (self.ring[0, 0] + self.ring[1, 0])

    def drain(self):
        for d in range(self.n):
            self.pair_copy(d).wait_send()
        for way in (0, 1):
            for q in range(self.pieces):
                self.ring_copy(way, q).wait_send()


class Gather:
    def __init__(self, place, full, rows, rsend, rrecv, fsend, frecv):
        self.pl, self.full, self.rows = place, full, rows
        self.rsend, self.rrecv, self.fsend, self.frecv = rsend, rrecv, fsend, frecv
        self.half_rows = rows // 2
        self.n = place.chips
        self.pieces = self.n - 1

    def piece(self, way, q, core, lag):
        hop = q // 2 + lag
        chip = self.pl.at(-hop if way == 0 else hop)
        half = way if q % 2 == 0 else 1 - way
        row = (chip * 2 + core) * self.rows + half * self.half_rows
        return self.full.at[ds(row, self.half_rows, 16), :]

    def ring_copy(self, way, q):
        ref = self.piece(way, q, self.pl.core, 0)
        return remote(ref, ref, self.rsend.at[way, q], self.rrecv.at[way, q], self.pl.next(way))

    def arrival(self, way, q):
        ref = self.piece(way, q, self.pl.core, 1)
        return remote(ref, ref, self.rsend.at[way, q], self.rrecv.at[way, q], self.pl.next(way))

    def forward(self, way, q, core):
        ref = self.piece(way, q, core, 1)
        return remote(ref, ref, self.fsend.at[way, q], self.frecv.at[way, q], self.pl.partner)

    def own_rows(self, core):
        return self.full.at[ds((self.pl.chip * 2 + core) * self.rows, self.rows, 32), :]

    def forward_own(self, core):
        ref = self.own_rows(core)
        return remote(ref, ref, self.fsend.at[0, self.pieces], self.frecv.at[0, self.pieces], self.pl.partner)

    def step(self, q):
        if q == 0:
            for k in (0, 1):
                for way in (0, 1):
                    self.ring_copy(way, k).start()
            self.forward_own(self.pl.core).start()
        else:
            for way in (0, 1):
                self.arrival(way, q - 1).wait_recv()
                if q + 1 < self.pieces:
                    self.ring_copy(way, q + 1).start()
                self.forward(way, q - 1, self.pl.core).start()

    def steps(self):
        return self.pieces + 1

    def finish(self):
        self.forward_own(1 - self.pl.core).wait_recv()
        for way in (0, 1):
            for q in range(self.pieces):
                self.forward(way, q, 1 - self.pl.core).wait_recv()

    def drain(self):
        self.forward_own(self.pl.core).wait_send()
        for way in (0, 1):
            for q in range(self.pieces):
                self.forward(way, q, self.pl.core).wait_send()
                self.ring_copy(way, q).wait_send()


def squares(mat):
    sq = mat * mat
    rows, cols = mat.shape
    acc = sq[0:8]
    for i in range(1, rows // 8):
        acc = acc + sq[8 * i:8 * i + 8]
    out = acc[:, 0:128]
    for j in range(1, cols // 128):
        out = out + acc[:, 128 * j:128 * j + 128]
    return out


def total_norm(ref, top):
    acc = ref[0, top:top + 8]
    for i in range(1, ref.shape[0]):
        acc = acc + ref[i, top:top + 8]
    total = jnp.sum(jnp.sum(acc, axis=1, keepdims=True), axis=0, keepdims=True)
    return jnp.sqrt(total) + EPSILON


def kernel(group, grads, moms, masters, outs, sc):
    place = Place(group)
    core, chip = place.core, place.chip
    chips = place.chips
    pieces = chips - 1
    barrier = pltpu.get_barrier_semaphore()
    for dev in (place.partner, place.next(0), place.next(1)):
        pl.semaphore_signal(barrier, inc=1, device_id={'data': dev}, device_id_type=pl.DeviceIdType.MESH)
    pl.semaphore_wait(barrier, 3)

    scat = [Scatter(place, grads[k], sc['own'][k], sc['pair'][k], sc['ring'][k], sc['load'].at[k], sc['psend'].at[k], sc['precv'].at[k],
                    sc['rsend'].at[k], sc['rrecv'].at[k]) for k in range(3)]
    fulls = [sc['x'].at[0], sc['tall'], sc['xu'].at[0]]
    gath = [Gather(place, fulls[k], sc['own'][k].shape[1], sc['gsend'].at[k], sc['grecv'].at[k], sc['fsend'].at[k], sc['frecv'].at[k]) for k in range(3)]

    scat[0].start()
    in_copies = []
    for k in range(3):
        in_copies.append((pltpu.make_async_copy(moms[k], sc['mom'][k], sc['insem'].at[k]),
                          pltpu.make_async_copy(masters[k], sc['master'][k], sc['insem'].at[3 + k])))
    for pair in in_copies:
        for copy in pair:
            copy.start()
    scat[1].start()
    scat[2].start()

    def out_copy(k, j, ref):
        return pltpu.make_async_copy(ref, outs[3 * k + j], sc['outsem'].at[3 * k + j])

    def momentum(k):
        in_copies[k][0].wait()
        mat = MOMENTUM * sc['mom'][k][...] + scat[k].total() * (1.0 / group)
        sc['mom'][k][...] = mat
        out_copy(k, 0, sc['mom'][k]).start()
        return squares(mat)

    def norm_copy(idx, i):
        ref = sc['norm'][idx]
        dev = lax.rem(place.me + i, group)
        return remote(ref.at[0], ref.at[i], sc['nsend'].at[idx, i], sc['nrecv'].at[idx, i], dev)

    def norm_send(idx):
        for i in range(1, group):
            norm_copy(idx, i).start()

    def norm_wait(idx):
        for i in range(1, group):
            norm_copy(idx, i).wait_recv()

    def norm_drain(idx):
        for i in range(1, group):
            norm_copy(idx, i).wait_send()

    def write_x(k, norm):
        rows = sc['own'][k].shape[1]
        fulls[k][ds((chip * 2 + core) * rows, rows, 32), :] = (sc['mom'][k][...] / norm).astype(BF16)

    for q in range(pieces):
        scat[0].step(q)
    sc['norm'][0][0] = momentum(0)
    norm_send(0)
    for q in (0, 1):
        for k in (1, 2):
            scat[k].step(q)
    norm_wait(0)
    write_x(0, total_norm(sc['norm'][0], 0))
    for q in range(gath[0].steps()):
        gath[0].step(q)
    gath[0].finish()

    tasks = {}

    def background(it, slot, fn):
        tasks.setdefault((it, slot), []).append(fn)

    def ud_momentum():
        sc['norm'][1][0, 0:8] = momentum(1)
        sc['norm'][1][0, 8:16] = momentum(2)
        norm_send(1)

    def ud_write():
        norm_wait(1)
        write_x(1, total_norm(sc['norm'][1], 0))
        write_x(2, total_norm(sc['norm'][1], 8))

    def both(parts, q):
        def run():
            parts[1].step(q)
            parts[2].step(q)
        return run

    background(0, 1, gath[0].drain)
    times = [(0, 3), (0, 5), (1, 1), (1, 3), (1, 5)]
    for q in range(2, pieces):
        background(*times[q - 2], both(scat, q))
    background(2, 0, ud_momentum)
    background(2, 1, ud_write)
    times = [(2, 1), (2, 2), (2, 3), (2, 4), (3, 0), (3, 2), (3, 3), (3, 4)]
    for q in range(gath[1].steps()):
        background(*times[q], both(gath, q))

    x, a, b, qacc = sc['x'], sc['a'], sc['b'], sc['qacc']
    size = x.shape[1]
    half = size // 2
    mine = ds(core * half, half, 128)
    theirs = ds((1 - core) * half, half, 128)

    def a_copy(i):
        if i == 0:
            return remote(a.at[mine, mine], a.at[mine, mine], sc['asend'].at[0], sc['arecv'].at[0], place.partner)
        rows = ds(core * half + (i - 1) * (half // 2), half // 2, 128)
        return remote(a.at[rows, theirs], a.at[rows, theirs], sc['asend'].at[i], sc['arecv'].at[i], place.partner)

    def x_copy(buf, n):
        ref = x.at[buf, mine, pl.ds(n * half, half)]
        return remote(ref, ref, sc['xsend'].at[n], sc['xrecv'].at[n], place.partner)

    def ns_step(it, carry):
        cur = lax.rem(it, 2)
        nxt = 1 - cur

        def slot(s):
            for (t, u), fns in tasks.items():
                if u == s:
                    def run(fns=fns):
                        for fn in fns:
                            fn()
                    pl.when(it == t)(run)

        slot(0)
        a[mine, mine] = dot_nt(x[cur, mine, :], x[cur, mine, :]).astype(BF16)
        slot(1)

        @pl.when(it > 0)
        def _():
            for n in (0, 1):
                x_copy(cur, n).wait_recv()
                x_copy(cur, n).wait_send()

        a_copy(0).start()
        for i in (0, 1):
            rows = ds(core * half + i * (half // 2), half // 2, 128)
            a[rows, theirs] = dot_nt(x[cur, rows, :], x[cur, theirs, :]).astype(BF16)
            a_copy(1 + i).start()
        slot(2)

        @pl.when(it < NS_STEPS - 1)
        def _():
            for n in (0, 1):
                cols = pl.ds(n * half, half)
                qacc[:, cols] = dot_nn(a[mine, mine], a[mine, cols])

        slot(3)
        for i in range(3):
            a_copy(i).wait_recv()

        @pl.when(it < NS_STEPS - 1)
        def _():
            for n in (0, 1):
                cols = pl.ds(n * half, half)
                acc = qacc[:, cols] + dot_nn(a[mine, theirs], a[theirs, cols])
                b[:, cols] = (COEF_B * a[mine, cols].astype(F32) + COEF_C * acc.astype(BF16).astype(F32)).astype(BF16)

        slot(4)
        for i in range(3):
            a_copy(i).wait_send()

        @pl.when(it < NS_STEPS - 1)
        def _():
            for n in (0, 1):
                cols = pl.ds(n * half, half)
                upd = dot_nn(b[...], x[cur, :, cols])
                x[nxt, mine, cols] = (COEF_A * x[cur, mine, cols].astype(F32) + upd.astype(BF16).astype(F32)).astype(BF16)
                x_copy(nxt, n).start()

        slot(5)
        return carry

    lax.fori_loop(0, NS_STEPS, ns_step, 0)

    def finish(k, ortho, scale):
        in_copies[k][1].wait()
        old = sc['master'][k][...]
        new = old - LEARN_RATE * (scale * ortho.astype(F32) + WEIGHT_DECAY * old)
        sc['master'][k][...] = new
        out_copy(k, 1, sc['master'][k]).start()
        sc['weight'][k][...] = new.astype(BF16)
        out_copy(k, 2, sc['weight'][k]).start()

    last = (NS_STEPS - 1) % 2
    rows_local = sc['own'][0].shape[1]
    own_rows = ds((chip * 2 + core) * rows_local, rows_local, 32)
    for n in (0, 1):
        cols = pl.ds(n * half, half)
        acc = dot_nn(a[own_rows, :], a[:, cols])
        b[0:rows_local, cols] = (COEF_B * a[own_rows, cols].astype(F32) + COEF_C * acc.astype(BF16).astype(F32)).astype(BF16)
    upd = dot_nn(b[0:rows_local, :], x[last])
    ortho = (COEF_A * x[last, own_rows, :].astype(F32) + upd.astype(BF16).astype(F32)).astype(BF16)
    finish(0, ortho, 0.2 * math.sqrt(size))

    for k in (1, 2):
        gath[k].finish()
        gath[k].drain()
    xu, tall, bu = sc['xu'], sc['tall'], sc['bu']
    small, wide = xu.shape[1], xu.shape[2]
    block = 256

    @pl.when(core == 0)
    def _():
        def flip(i, carry):
            rows = ds(i * block, block, block)
            xu[0, :, rows] = tall[rows, :].astype(F32).T.astype(BF16)
            return carry
        lax.fori_loop(0, wide // block, flip, 0)

    def ud_step(it, carry):
        cur = lax.rem(it, 2)
        nxt = 1 - cur
        gram = dot_nt(xu[cur], xu[cur]).astype(BF16)
        bu[0] = gram
        sq = dot_nn(bu[0], bu[0]).astype(BF16)
        bu[1] = (COEF_B * bu[0].astype(F32) + COEF_C * sq.astype(F32)).astype(BF16)
        for n in (0, 1):
            cols = pl.ds(n * (wide // 2), wide // 2)
            upd = dot_nn(bu[1], xu[cur, :, cols])
            xu[nxt, :, cols] = (COEF_A * xu[cur, :, cols].astype(F32) + upd.astype(BF16).astype(F32)).astype(BF16)
        return carry

    lax.fori_loop(0, NS_STEPS, ud_step, 0)
    end = NS_STEPS % 2
    up_rows, down_rows = sc['own'][1].shape[1], sc['own'][2].shape[1]
    ou, od = sc['ou'], sc['od']
    up_ref = tall.at[ds((chip * 2 + 1) * up_rows, up_rows, 32), :]
    up_copy = remote(up_ref, ou, sc['osend'].at[0], sc['orecv'].at[0], place.partner)
    down_ref = xu.at[end, ds(chip * 2 * down_rows, down_rows, 32), :]
    down_copy = remote(down_ref, od, sc['osend'].at[1], sc['orecv'].at[1], place.partner)

    @pl.when(core == 0)
    def _():
        def flip(i, carry):
            rows = ds(i * block, block, block)
            tall[rows, :] = xu[end, :, rows].astype(F32).T.astype(BF16)
            return carry
        lax.fori_loop(0, wide // block, flip, 0)
        up_copy.start()
        ou[...] = tall[ds(chip * 2 * up_rows, up_rows, 32), :]
        down_copy.wait_recv()
        up_copy.wait_send()

    @pl.when(core == 1)
    def _():
        down_copy.start()
        od[...] = xu[end, ds((chip * 2 + 1) * down_rows, down_rows, 32), :]
        up_copy.wait_recv()
        down_copy.wait_send()

    finish(1, ou[...], 0.2 * math.sqrt(wide))
    finish(2, od[...], 0.2 * math.sqrt(wide))

    for k in range(3):
        scat[k].drain()
    norm_drain(0)
    norm_drain(1)
    for k in range(3):
        out_copy(k, 0, sc['mom'][k]).wait()
        out_copy(k, 1, sc['master'][k]).wait()
        out_copy(k, 2, sc['weight'][k]).wait()


def solution(mesh):
    group = mesh.shape['data']
    chips = group // 2
    pieces = chips - 1
    grad_spec = P(('stage', 'data'), None, None, None)
    row_spec = P('stage', 'data', None)

    def step_local(*arrays):
        grads = [arrays[3 * k].reshape(arrays[3 * k].shape[2:]) for k in range(3)]
        moms = [arrays[3 * k + 1].reshape(arrays[3 * k + 1].shape[1:]) for k in range(3)]
        masters = [arrays[3 * k + 2].reshape(arrays[3 * k + 2].shape[1:]) for k in range(3)]
        shapes = [m.shape for m in moms]
        size = grads[0].shape[0]
        wide, small = grads[1].shape
        dma = pltpu.SemaphoreType.DMA
        names, scratch = [], []

        def add(name, item):
            names.append(name)
            scratch.append(item)

        for k, (rows, cols) in enumerate(shapes):
            add(('own', k), pltpu.VMEM((chips, rows, cols), F32))
            add(('pair', k), pltpu.VMEM((chips, rows, cols), F32))
            add(('ring', k), pltpu.VMEM((2, chips // 2, rows, cols), F32))
            add(('mom', k), pltpu.VMEM((rows, cols), F32))
            add(('master', k), pltpu.VMEM((rows, cols), F32))
            add(('weight', k), pltpu.VMEM((rows, cols), BF16))
        add('x', pltpu.VMEM((2, size, size), BF16))
        add('a', pltpu.VMEM((size, size), BF16))
        add('b', pltpu.VMEM((size // 2, size), BF16))
        add('qacc', pltpu.VMEM((size // 2, size), F32))
        add('tall', pltpu.VMEM((wide, small), BF16))
        add('xu', pltpu.VMEM((2, small, wide), BF16))
        add('bu', pltpu.VMEM((2, small, small), BF16))
        add('ou', pltpu.VMEM(shapes[1], BF16))
        add('od', pltpu.VMEM(shapes[2], BF16))
        add(('norm', 0), pltpu.VMEM((group, 8, 128), F32))
        add(('norm', 1), pltpu.VMEM((group, 16, 128), F32))
        for name, shape in (('load', (3, chips)), ('psend', (3, chips)), ('precv', (3, chips)), ('rsend', (3, 2, pieces)), ('rrecv', (3, 2, pieces)),
                            ('gsend', (3, 2, pieces)), ('grecv', (3, 2, pieces)), ('fsend', (3, 2, chips)), ('frecv', (3, 2, chips)),
                            ('nsend', (2, group)), ('nrecv', (2, group)), ('insem', (6,)), ('outsem', (9,)), ('asend', (3,)), ('arecv', (3,)),
                            ('xsend', (2,)), ('xrecv', (2,)), ('osend', (2,)), ('orecv', (2,))):
            add(name, dma(shape))

        def body(*refs):
            sc = {}
            for name, ref in zip(names, refs[18:]):
                if isinstance(name, tuple):
                    sc.setdefault(name[0], []).append(ref)
                else:
                    sc[name] = ref
            kernel(group, refs[0:3], refs[3:6], refs[6:9], refs[9:18], sc)

        out_shape = []
        for shape in shapes:
            out_shape += [jax.ShapeDtypeStruct(shape, F32), jax.ShapeDtypeStruct(shape, F32), jax.ShapeDtypeStruct(shape, BF16)]
        results = pl.pallas_call(
            body,
            out_shape=tuple(out_shape),
            in_specs=[pl.BlockSpec(memory_space=pl.ANY)] * 9,
            out_specs=tuple([pl.BlockSpec(memory_space=pl.ANY)] * 9),
            scratch_shapes=scratch,
            compiler_params=pltpu.CompilerParams(collective_id=0, has_side_effects=True, vmem_limit_bytes=64 * 1024 * 1024 - 65536),
            name='muon',
        )(*grads, *moms, *masters)
        return tuple(r[None] for r in results)

    in_specs = (grad_spec, row_spec, row_spec) * 3
    out_specs = (row_spec,) * 9
    return jax.shard_map(step_local, mesh=mesh, in_specs=in_specs, out_specs=out_specs, check_vma=False)
```

time: 876 us -> 208 us (0.24); the launches traced: 866 us -> 208 us
  waiting for transfers between devices: 412 us -> 0 us
  starting transfers between devices: 222 us -> 0 us
  Pallas kernels: 0 us -> 197 us
  local copies, waits for them, and re-layouts: 91.6 us -> 10.5 us
  other arithmetic: 63.9 us -> 0 us
  matrix products: 26.9 us -> 0 us
  blocking collectives: 26.9 us -> 0 us
  between operations: 16.3 us -> 0.7 us
    all_to_all x6 -> x0, waiting for transfers between devices: 223 us -> none  [the longest x3 119 us: stack_step(): lax.all_to_all(ortho_mat.reshape(slots, 1, n_rows, n_cols), 'data', 2, 1,...]
    all_to_all x6 -> x0, starting transfers between devices: 222 us -> none  [the longest x3 205 us: stack_step(): lax.all_to_all(ortho_mat.reshape(slots, 1, n_rows, n_cols), 'data', 2, 1,...]
    pallas_call x0 -> x1, Pallas kernels: none -> 197 us  [step_local(): pl.pallas_call(body, out_shape=tuple(out_shape), in_specs=[pl.BlockSpec(m...]
    reduce_scatter x3 -> x0, waiting for transfers between devices: 188 us -> none  [stack_step(): lax.psum_scatter(grad_all[0], 'data', scatter_dimension=1, tiled=True)]
    unnamed x3 -> x0, other arithmetic: 54.7 us -> none
    unnamed x34 -> x19, local copies, waits for them, and re-layouts: 61.8 us -> 10.5 us
    reshape x7 -> x0, local copies, waits for them, and re-layouts: 27.3 us -> none  [the longest x3 20.3 us: stack_step(): ortho_mat.reshape(slots, 1, n_rows, n_cols)]
    dot_general x10 -> x0, matrix products: 26.9 us -> none  [the longest x5 14.7 us: newton_schulz(): jnp.einsum('bkc,brc->bkr', x_mat, poly_mat, preferred_element_type=jnp.fl...]
  transfers between devices with their start and end apart: 9 -> 0, of which waited for: 8 -> 0; matrix products, arithmetic and copies ran while one was open for 18% -> 0% of each run, Pallas kernels for 0% -> 0%
where the time goes in v1:
time: 208 us
  Pallas kernels  197 us (95%)
  local copies, waits for them, and re-layouts  10.5 us (5%)
    pallas_call x1, Pallas kernels, step_local(): pl.pallas_call(body, out_shape=tuple(out_shape), in_specs=[pl.BlockSpec(m...  197 us
    unnamed x19, local copies, waits for them, and re-layouts  10.5 us

profile of v1, /device:TPU:21, one launch (start us, length us, event | category | flops | bytes accessed | tf_op | source)
XLA Modules:
  0.0 207.9 jit_solution(4231588154245250662)
XLA Ops:
  0.6 196.6 %muon.1 = (f32[96,1536]{1,0:T(8,128)}, f32[96,1536]{1,0:T(8,128)}, bf16[96,1536]{1,0:T(8,128)(2,1)}, f32[96,512]{1,0:T(8,128)}, f32[96,512]{1,0:T(8,128)}, /*ind...) custom-call(f32[1536,1536]{1,0:T(8,128)} %bitcast.18, ...), custom_call_target="tpu_custom_call" | custom-call | tf_op jit(solution)/shard_map/muon/pallas_call | solution.py:535
  197.3 0.0 copy-start.2
  197.3 0.0 copy-start.4
  197.3 0.0 copy-start.1
  197.3 0.0 copy-start
  197.3 0.0 copy-start.3
  197.3 2.0 copy.27
  199.3 1.9 copy.28
  201.2 1.7 copy.29
  202.9 1.6 copy.30
  204.5 0.0 copy-done.2
  204.5 0.7 copy.31
  205.2 0.0 copy-done.4
  205.2 0.6 copy.32
  205.9 0.0 copy-done.1
  205.9 0.7 copy.33
  206.5 0.0 copy-done
  206.5 0.7 copy.34
  207.2 0.0 copy-done.3
  207.2 0.6 copy.35
Async XLA Ops:
  197.3 7.3 %copy-start.2 = (f32[96,512]{1,0:T(8,128)S(1)}, f32[96,512]{1,0:T(8,128)}, u32[]{:S(2)}) copy-start(f32[96,512]{1,0:T(8,128)} %get-tuple-element.22) | copy-start | bytes 589828
  197.3 7.9 %copy-start.4 = (bf16[96,512]{1,0:T(8,128)(2,1)S(1)}, bf16[96,512]{1,0:T(8,128)(2,1)}, u32[]{:S(2)}) copy-start(bf16[96,512]{1,0:T(8,128)(2,1)} %get-tuple-element.23) | copy-start | bytes 294916
  197.3 8.6 %copy-start.1 = (f32[32,1536]{1,0:T(8,128)S(1)}, f32[32,1536]{1,0:T(8,128)}, u32[]{:S(2)}) copy-start(f32[32,1536]{1,0:T(8,128)} %get-tuple-element.24) | copy-start | bytes 589828
  197.3 9.2 %copy-start = (f32[32,1536]{1,0:T(8,128)S(1)}, f32[32,1536]{1,0:T(8,128)}, u32[]{:S(2)}) copy-start(f32[32,1536]{1,0:T(8,128)} %get-tuple-element.25) | copy-start | bytes 589828
  197.3 9.9 %copy-start.3 = (bf16[32,1536]{1,0:T(8,128)(2,1)S(1)}, bf16[32,1536]{1,0:T(8,128)(2,1)}, u32[]{:S(2)}) copy-start(bf16[32,1536]{1,0:T(8,128)(2,1)} %get-tuple-element.26) | copy-start | bytes 294916

commit v2 on v1

--- a/solution.py
+++ b/solution.py
@@ -21,6 +21,10 @@
 
 def dot_nn(a, b):
     return lax.dot_general(a, b, (((1,), (0,)), ((), ())), preferred_element_type=F32)
+
+
+def dot_tn(a, b):
+    return lax.dot_general(a, b, (((0,), (0,)), ((), ())), preferred_element_type=F32)
 
 
 def dot_nt(a, b):
@@ -123,18 +127,21 @@
 
 
 class Gather:
-    def __init__(self, place, full, rows, rsend, rrecv, fsend, frecv):
-        self.pl, self.full, self.rows = place, full, rows
+    def __init__(self, place, full, rows, panels, rsend, rrecv, fsend, frecv):
+        self.pl, self.full, self.rows, self.panels = place, full, rows, panels
         self.rsend, self.rrecv, self.fsend, self.frecv = rsend, rrecv, fsend, frecv
         self.half_rows = rows // 2
         self.n = place.chips
         self.pieces = self.n - 1
 
+    def base(self, chip, core):
+        return ((core * self.n + chip) if self.panels else (chip * 2 + core)) * self.rows
+
     def piece(self, way, q, core, lag):
         hop = q // 2 + lag
         chip = self.pl.at(-hop if way == 0 else hop)
         half = way if q % 2 == 0 else 1 - way
-        row = (chip * 2 + core) * self.rows + half * self.half_rows
+        row = self.base(chip, core) + half * self.half_rows
         return self.full.at[ds(row, self.half_rows, 16), :]
 
     def ring_copy(self, way, q):
@@ -150,7 +157,7 @@
         return remote(ref, ref, self.fsend.at[way, q], self.frecv.at[way, q], self.pl.partner)
 
     def own_rows(self, core):
-        return self.full.at[ds((self.pl.chip * 2 + core) * self.rows, self.rows, 32), :]
+        return self.full.at[ds(self.base(self.pl.chip, core), self.rows, 32), :]
 
     def forward_own(self, core):
         ref = self.own_rows(core)
@@ -206,7 +213,7 @@
     return jnp.sqrt(total) + EPSILON
 
 
-def kernel(group, grads, moms, masters, outs, sc):
+def kernel(group, grads, moms, outs, sc):
     place = Place(group)
     core, chip = place.core, place.chip
     chips = place.chips
@@ -218,25 +225,22 @@
 
     scat = [Scatter(place, grads[k], sc['own'][k], sc['pair'][k], sc['ring'][k], sc['load'].at[k], sc['psend'].at[k], sc['precv'].at[k],
                     sc['rsend'].at[k], sc['rrecv'].at[k]) for k in range(3)]
-    fulls = [sc['x'].at[0], sc['tall'], sc['xu'].at[0]]
-    gath = [Gather(place, fulls[k], sc['own'][k].shape[1], sc['gsend'].at[k], sc['grecv'].at[k], sc['fsend'].at[k], sc['frecv'].at[k]) for k in range(3)]
+    fulls = [sc['x'][0], sc['tall'], sc['xd']]
+    gath = [Gather(place, fulls[k], sc['own'][k].shape[1], k == 0, sc['gsend'].at[k], sc['grecv'].at[k], sc['fsend'].at[k], sc['frecv'].at[k]) for k in range(3)]
 
     scat[0].start()
     in_copies = []
     for k in range(3):
-        in_copies.append((pltpu.make_async_copy(moms[k], sc['mom'][k], sc['insem'].at[k]),
-                          pltpu.make_async_copy(masters[k], sc['master'][k], sc['insem'].at[3 + k])))
-    for pair in in_copies:
-        for copy in pair:
-            copy.start()
+        in_copies.append(pltpu.make_async_copy(moms[k], sc['mom'][k], sc['insem'].at[k]))
+        in_copies[k].start()
     scat[1].start()
     scat[2].start()
 
     def out_copy(k, j, ref):
-        return pltpu.make_async_copy(ref, outs[3 * k + j], sc['outsem'].at[3 * k + j])
+        return pltpu.make_async_copy(ref, outs[2 * k + j], sc['outsem'].at[2 * k + j])
 
     def momentum(k):
-        in_copies[k][0].wait()
+        in_copies[k].wait()
         mat = MOMENTUM * sc['mom'][k][...] + scat[k].total() * (1.0 / group)
         sc['mom'][k][...] = mat
         out_copy(k, 0, sc['mom'][k]).start()
@@ -261,7 +265,7 @@
 
     def write_x(k, norm):
         rows = sc['own'][k].shape[1]
-        fulls[k][ds((chip * 2 + core) * rows, rows, 32), :] = (sc['mom'][k][...] / norm).astype(BF16)
+        fulls[k][ds(gath[k].base(chip, core), rows, 32), :] = (sc['mom'][k][...] / norm).astype(BF16)
 
     for q in range(pieces):
         scat[0].step(q)
@@ -274,7 +278,9 @@
     write_x(0, total_norm(sc['norm'][0], 0))
     for q in range(gath[0].steps()):
         gath[0].step(q)
-    gath[0].finish()
+        if q + 2 == pieces:
+            for k in (1, 2):
+                scat[k].step(2)
 
     tasks = {}
 
@@ -297,19 +303,19 @@
             parts[2].step(q)
         return run
 
-    background(0, 1, gath[0].drain)
-    times = [(0, 3), (0, 5), (1, 1), (1, 3), (1, 5)]
-    for q in range(2, pieces):
-        background(*times[q - 2], both(scat, q))
-    background(2, 0, ud_momentum)
-    background(2, 1, ud_write)
-    times = [(2, 1), (2, 2), (2, 3), (2, 4), (3, 0), (3, 2), (3, 3), (3, 4)]
+    background(0, 0, both(scat, 3))
+    for q, place_at in ((4, (0, 3)), (5, (0, 5)), (6, (1, 1))):
+        background(*place_at, both(scat, q))
+    background(1, 5, ud_momentum)
+    background(2, 2, ud_write)
+    times = ((2, 2), (2, 5), (2, 6), (3, 1), (3, 2), (3, 3), (3, 5), (3, 6))
     for q in range(gath[1].steps()):
         background(*times[q], both(gath, q))
 
-    x, a, b, qacc = sc['x'], sc['a'], sc['b'], sc['qacc']
-    size = x.shape[1]
+    xs, a, b, qacc = sc['x'], sc['a'], sc['b'], sc['qacc']
+    size = a.shape[0]
     half = size // 2
+    third = size // 3
     mine = ds(core * half, half, 128)
     theirs = ds((1 - core) * half, half, 128)
 
@@ -319,151 +325,158 @@
         rows = ds(core * half + (i - 1) * (half // 2), half // 2, 128)
         return remote(a.at[rows, theirs], a.at[rows, theirs], sc['asend'].at[i], sc['arecv'].at[i], place.partner)
 
-    def x_copy(buf, n):
-        ref = x.at[buf, mine, pl.ds(n * half, half)]
+    def x_copy(x, n):
+        ref = x.at[mine, pl.ds(n * third, third)]
         return remote(ref, ref, sc['xsend'].at[n], sc['xrecv'].at[n], place.partner)
 
-    def ns_step(it, carry):
-        cur = lax.rem(it, 2)
-        nxt = 1 - cur
+    def x_wait(x):
+        for n in range(3):
+            x_copy(x, n).wait_recv()
+            x_copy(x, n).wait_send()
+
+    def grams(x, slot, wait):
+        slot(0)
+        a[mine, mine] = dot_nt(x[mine, :], x[mine, :]).astype(BF16)
+        wait()
+        slot(1)
+        a_copy(0).start()
+        for i in (0, 1):
+            rows = ds(core * half + i * (half // 2), half // 2, 128)
+            a[rows, theirs] = dot_nt(x[rows, :], x[theirs, :]).astype(BF16)
+            a_copy(1 + i).start()
+
+    def a_wait():
+        for i in range(3):
+            a_copy(i).wait_recv()
+
+    def a_drain():
+        for i in range(3):
+            a_copy(i).wait_send()
+
+    def poly(lin, acc):
+        return (COEF_B * lin.astype(F32) + COEF_C * acc.astype(BF16).astype(F32)).astype(BF16)
+
+    def renew(old, upd):
+        return (COEF_A * old.astype(F32) + upd.astype(BF16).astype(F32)).astype(BF16)
+
+    def ns_step(pair, parity):
+        x, xn = xs[parity], xs[1 - parity]
 
         def slot(s):
             for (t, u), fns in tasks.items():
-                if u == s:
+                if u == s and t % 2 == parity:
                     def run(fns=fns):
                         for fn in fns:
                             fn()
-                    pl.when(it == t)(run)
-
-        slot(0)
-        a[mine, mine] = dot_nt(x[cur, mine, :], x[cur, mine, :]).astype(BF16)
-        slot(1)
-
-        @pl.when(it > 0)
-        def _():
-            for n in (0, 1):
-                x_copy(cur, n).wait_recv()
-                x_copy(cur, n).wait_send()
-
-        a_copy(0).start()
-        for i in (0, 1):
-            rows = ds(core * half + i * (half // 2), half // 2, 128)
-            a[rows, theirs] = dot_nt(x[cur, rows, :], x[cur, theirs, :]).astype(BF16)
-            a_copy(1 + i).start()
+                    pl.when(pair == t // 2)(run)
+
+        def wait():
+            if parity == 0:
+                @pl.when(pair == 0)
+                def _():
+                    gath[0].finish()
+                    gath[0].drain()
+
+                @pl.when(pair > 0)
+                def _():
+                    x_wait(x)
+            else:
+                x_wait(x)
+
+        grams(x, slot, wait)
         slot(2)
-
-        @pl.when(it < NS_STEPS - 1)
-        def _():
-            for n in (0, 1):
-                cols = pl.ds(n * half, half)
-                qacc[:, cols] = dot_nn(a[mine, mine], a[mine, cols])
-
+        for n in (0, 1):
+            cols = pl.ds(n * half, half)
+            qacc[:, cols] = dot_nn(a[mine, mine], a[mine, cols])
         slot(3)
-        for i in range(3):
-            a_copy(i).wait_recv()
-
-        @pl.when(it < NS_STEPS - 1)
-        def _():
-            for n in (0, 1):
-                cols = pl.ds(n * half, half)
-                acc = qacc[:, cols] + dot_nn(a[mine, theirs], a[theirs, cols])
-                b[:, cols] = (COEF_B * a[mine, cols].astype(F32) + COEF_C * acc.astype(BF16).astype(F32)).astype(BF16)
-
+        a_wait()
+        for n in (0, 1):
+            cols = pl.ds(n * half, half)
+            b[:, cols] = poly(a[mine, cols], qacc[:, cols] + dot_nn(a[mine, theirs], a[theirs, cols]))
         slot(4)
-        for i in range(3):
-            a_copy(i).wait_send()
-
-        @pl.when(it < NS_STEPS - 1)
-        def _():
-            for n in (0, 1):
-                cols = pl.ds(n * half, half)
-                upd = dot_nn(b[...], x[cur, :, cols])
-                x[nxt, mine, cols] = (COEF_A * x[cur, mine, cols].astype(F32) + upd.astype(BF16).astype(F32)).astype(BF16)
-                x_copy(nxt, n).start()
-
-        slot(5)
+        a_drain()
+        for n in range(3):
+            cols = pl.ds(n * third, third)
+            xn[mine, cols] = renew(x[mine, cols], dot_nn(b[...], x[:, cols]))
+            x_copy(xn, n).start()
+            if n < 2:
+                slot(5 + n)
+
+    def ns_pair(pair, carry):
+        ns_step(pair, 0)
+        ns_step(pair, 1)
         return carry
 
-    lax.fori_loop(0, NS_STEPS, ns_step, 0)
-
-    def finish(k, ortho, scale):
-        in_copies[k][1].wait()
-        old = sc['master'][k][...]
-        new = old - LEARN_RATE * (scale * ortho.astype(F32) + WEIGHT_DECAY * old)
-        sc['master'][k][...] = new
-        out_copy(k, 1, sc['master'][k]).start()
-        sc['weight'][k][...] = new.astype(BF16)
-        out_copy(k, 2, sc['weight'][k]).start()
-
-    last = (NS_STEPS - 1) % 2
+    lax.fori_loop(0, NS_STEPS // 2, ns_pair, 0)
+
+    x = xs[0]
+    grams(x, lambda s: None, lambda: x_wait(x))
+    a_wait()
     rows_local = sc['own'][0].shape[1]
-    own_rows = ds((chip * 2 + core) * rows_local, rows_local, 32)
+    own_rows = ds(core * half + chip * rows_local, rows_local, 32)
     for n in (0, 1):
         cols = pl.ds(n * half, half)
-        acc = dot_nn(a[own_rows, :], a[:, cols])
-        b[0:rows_local, cols] = (COEF_B * a[own_rows, cols].astype(F32) + COEF_C * acc.astype(BF16).astype(F32)).astype(BF16)
-    upd = dot_nn(b[0:rows_local, :], x[last])
-    ortho = (COEF_A * x[last, own_rows, :].astype(F32) + upd.astype(BF16).astype(F32)).astype(BF16)
-    finish(0, ortho, 0.2 * math.sqrt(size))
+        b[0:rows_local, cols] = poly(a[own_rows, cols], dot_nn(a[own_rows, :], a[:, cols]))
+    a_drain()
+    sc['oa'][...] = renew(x[own_rows, :], dot_nn(b[0:rows_local, :], x[...]))
+    out_copy(0, 1, sc['oa']).start()
 
     for k in (1, 2):
         gath[k].finish()
         gath[k].drain()
-    xu, tall, bu = sc['xu'], sc['tall'], sc['bu']
-    small, wide = xu.shape[1], xu.shape[2]
-    block = 256
+    xd, tall, bu = sc['xd'], sc['tall'], sc['bu']
+    small, wide = xd.shape
+    up_rows, down_rows = sc['own'][1].shape[1], sc['own'][2].shape[1]
+    up_send, down_send = sc['up_send'], sc['down_send']
+    up_copy = remote(up_send, sc['ou'], sc['osend'].at[0], sc['orecv'].at[0], place.partner)
+    down_copy = remote(down_send, sc['od'], sc['osend'].at[1], sc['orecv'].at[1], place.partner)
+    half_wide = wide // 2
 
     @pl.when(core == 0)
     def _():
-        def flip(i, carry):
-            rows = ds(i * block, block, block)
-            xu[0, :, rows] = tall[rows, :].astype(F32).T.astype(BF16)
+        def step(it, carry):
+            bu[0] = dot_tn(tall[...], tall[...]).astype(BF16)
+            bu[1] = poly(bu[0], dot_nn(bu[0], bu[0]))
+            for n in (0, 1):
+                rows = pl.ds(n * half_wide, half_wide)
+                tall[rows, :] = renew(tall[rows, :], dot_nn(tall[rows, :], bu[1]))
             return carry
-        lax.fori_loop(0, wide // block, flip, 0)
-
-    def ud_step(it, carry):
-        cur = lax.rem(it, 2)
-        nxt = 1 - cur
-        gram = dot_nt(xu[cur], xu[cur]).astype(BF16)
-        bu[0] = gram
-        sq = dot_nn(bu[0], bu[0]).astype(BF16)
-        bu[1] = (COEF_B * bu[0].astype(F32) + COEF_C * sq.astype(F32)).astype(BF16)
-        for n in (0, 1):
-            cols = pl.ds(n * (wide // 2), wide // 2)
-            upd = dot_nn(bu[1], xu[cur, :, cols])
-            xu[nxt, :, cols] = (COEF_A * xu[cur, :, cols].astype(F32) + upd.astype(BF16).astype(F32)).astype(BF16)
-        return carry
-
-    lax.fori_loop(0, NS_STEPS, ud_step, 0)
-    end = NS_STEPS % 2
-    up_rows, down_rows = sc['own'][1].shape[1], sc['own'][2].shape[1]
-    ou, od = sc['ou'], sc['od']
-    up_ref = tall.at[ds((chip * 2 + 1) * up_rows, up_rows, 32), :]
-    up_copy = remote(up_ref, ou, sc['osend'].at[0], sc['orecv'].at[0], place.partner)
-    down_ref = xu.at[end, ds(chip * 2 * down_rows, down_rows, 32), :]
-    down_copy = remote(down_ref, od, sc['osend'].at[1], sc['orecv'].at[1], place.partner)
-
-    @pl.when(core == 0)
-    def _():
-        def flip(i, carry):
-            rows = ds(i * block, block, block)
-            tall[rows, :] = xu[end, :, rows].astype(F32).T.astype(BF16)
-            return carry
-        lax.fori_loop(0, wide // block, flip, 0)
+        lax.fori_loop(0, NS_STEPS - 1, step, 0)
+        bu[0] = dot_tn(tall[...], tall[...]).astype(BF16)
+        bu[1] = poly(bu[0], dot_nn(bu[0], bu[0]))
+        other = tall[ds((chip * 2 + 1) * up_rows, up_rows, 32), :]
+        up_send[...] = renew(other, dot_nn(other, bu[1]))
         up_copy.start()
-        ou[...] = tall[ds(chip * 2 * up_rows, up_rows, 32), :]
+        own = tall[ds(chip * 2 * up_rows, up_rows, 32), :]
+        sc['ou'][...] = renew(own, dot_nn(own, bu[1]))
+        out_copy(1, 1, sc['ou']).start()
         down_copy.wait_recv()
+        out_copy(2, 1, sc['od']).start()
         up_copy.wait_send()
 
     @pl.when(core == 1)
     def _():
+        def step(it, carry):
+            bu[0] = dot_nt(xd[...], xd[...]).astype(BF16)
+            bu[1] = poly(bu[0], dot_nn(bu[0], bu[0]))
+            for n in (0, 1):
+                cols = pl.ds(n * half_wide, half_wide)
+                xd[:, cols] = renew(xd[:, cols], dot_nn(bu[1], xd[:, cols]))
+            return carry
+        lax.fori_loop(0, NS_STEPS - 1, step, 0)
+        bu[0] = dot_nt(xd[...], xd[...]).astype(BF16)
+
+        def rows_of(which):
+            rows = ds((chip * 2 + which) * down_rows, down_rows, 32)
+            part = poly(bu[0, rows, :], dot_nn(bu[0, rows, :], bu[0]))
+            return renew(xd[rows, :], dot_nn(part, xd[...]))
+        down_send[...] = rows_of(0)
         down_copy.start()
-        od[...] = xu[end, ds((chip * 2 + 1) * down_rows, down_rows, 32), :]
+        sc['od'][...] = rows_of(1)
+        out_copy(2, 1, sc['od']).start()
         up_copy.wait_recv()
+        out_copy(1, 1, sc['ou']).start()
         down_copy.wait_send()
-
-    finish(1, ou[...], 0.2 * math.sqrt(wide))
-    finish(2, od[...], 0.2 * math.sqrt(wide))
 
     for k in range(3):
         scat[k].drain()
@@ -471,8 +484,18 @@
     norm_drain(1)
     for k in range(3):
         out_copy(k, 0, sc['mom'][k]).wait()
-        out_copy(k, 1, sc['master'][k]).wait()
-        out_copy(k, 2, sc['weight'][k]).wait()
+        out_copy(k, 1, sc[('oa', 'ou', 'od')[k]]).wait()
+
+
+def results_kernel(scales, *refs):
+    for k in range(3):
+        mom, ortho, master = refs[k], refs[3 + k], refs[6 + k]
+        mom_out, master_out, weight_out = refs[9 + 3 * k:12 + 3 * k]
+        mom_out[...] = mom[...]
+        old = master[...]
+        new = old - LEARN_RATE * (scales[k] * ortho[...].astype(F32) + WEIGHT_DECAY * old)
+        master_out[...] = new
+        weight_out[...] = new.astype(BF16)
 
 
 def solution(mesh):
@@ -501,46 +524,58 @@
             add(('pair', k), pltpu.VMEM((chips, rows, cols), F32))
             add(('ring', k), pltpu.VMEM((2, chips // 2, rows, cols), F32))
             add(('mom', k), pltpu.VMEM((rows, cols), F32))
-            add(('master', k), pltpu.VMEM((rows, cols), F32))
-            add(('weight', k), pltpu.VMEM((rows, cols), BF16))
-        add('x', pltpu.VMEM((2, size, size), BF16))
+        add(('x', 0), pltpu.VMEM((size, size), BF16))
+        add(('x', 1), pltpu.VMEM((size, size), BF16))
         add('a', pltpu.VMEM((size, size), BF16))
         add('b', pltpu.VMEM((size // 2, size), BF16))
         add('qacc', pltpu.VMEM((size // 2, size), F32))
         add('tall', pltpu.VMEM((wide, small), BF16))
-        add('xu', pltpu.VMEM((2, small, wide), BF16))
+        add('xd', pltpu.VMEM((small, wide), BF16))
         add('bu', pltpu.VMEM((2, small, small), BF16))
-        add('ou', pltpu.VMEM(shapes[1], BF16))
-        add('od', pltpu.VMEM(shapes[2], BF16))
+        for name, k in (('oa', 0), ('ou', 1), ('od', 2), ('up_send', 1), ('down_send', 2)):
+            add(name, pltpu.VMEM(shapes[k], BF16))
         add(('norm', 0), pltpu.VMEM((group, 8, 128), F32))
         add(('norm', 1), pltpu.VMEM((group, 16, 128), F32))
         for name, shape in (('load', (3, chips)), ('psend', (3, chips)), ('precv', (3, chips)), ('rsend', (3, 2, pieces)), ('rrecv', (3, 2, pieces)),
                             ('gsend', (3, 2, pieces)), ('grecv', (3, 2, pieces)), ('fsend', (3, 2, chips)), ('frecv', (3, 2, chips)),
-                            ('nsend', (2, group)), ('nrecv', (2, group)), ('insem', (6,)), ('outsem', (9,)), ('asend', (3,)), ('arecv', (3,)),
-                            ('xsend', (2,)), ('xrecv', (2,)), ('osend', (2,)), ('orecv', (2,))):
+                            ('nsend', (2, group)), ('nrecv', (2, group)), ('insem', (3,)), ('outsem', (6,)), ('asend', (3,)), ('arecv', (3,)),
+                            ('xsend', (3,)), ('xrecv', (3,)), ('osend', (2,)), ('orecv', (2,))):
             add(name, dma(shape))
 
         def body(*refs):
             sc = {}
-            for name, ref in zip(names, refs[18:]):
+            for name, ref in zip(names, refs[12:]):
                 if isinstance(name, tuple):
                     sc.setdefault(name[0], []).append(ref)
                 else:
                     sc[name] = ref
-            kernel(group, refs[0:3], refs[3:6], refs[6:9], refs[9:18], sc)
-
+            kernel(group, refs[0:3], refs[3:6], refs[6:12], sc)
+
+        anywhere = pl.BlockSpec(memory_space=pl.ANY)
+        part_shape = []
+        for shape in shapes:
+            part_shape += [jax.ShapeDtypeStruct(shape, F32), jax.ShapeDtypeStruct(shape, BF16)]
+        parts = pl.pallas_call(
+            body,
+            out_shape=tuple(part_shape),
+            in_specs=[anywhere] * 6,
+            out_specs=tuple([anywhere] * 6),
+            scratch_shapes=scratch,
+            compiler_params=pltpu.CompilerParams(collective_id=0, has_side_effects=True, vmem_limit_bytes=64 * 1024 * 1024 - 65536),
+            name='muon',
+        )(*grads, *moms)
+        scales = [0.2 * math.sqrt(max(g.shape)) for g in grads]
         out_shape = []
         for shape in shapes:
             out_shape += [jax.ShapeDtypeStruct(shape, F32), jax.ShapeDtypeStruct(shape, F32), jax.ShapeDtypeStruct(shape, BF16)]
+        vmem = pl.BlockSpec(memory_space=pltpu.VMEM)
         results = pl.pallas_call(
-            body,
+            functools.partial(results_kernel, scales),
             out_shape=tuple(out_shape),
-            in_specs=[pl.BlockSpec(memory_space=pl.ANY)] * 9,
-            out_specs=tuple([pl.BlockSpec(memory_space=pl.ANY)] * 9),
-            scratch_shapes=scratch,
-            compiler_params=pltpu.CompilerParams(collective_id=0, has_side_effects=True, vmem_limit_bytes=64 * 1024 * 1024 - 65536),
-            name='muon',
-        )(*grads, *moms, *masters)
+            in_specs=[vmem] * 9,
+            out_specs=tuple([vmem] * 9),
+            name='results',
+        )(*parts[0::2], *parts[1::2], *masters)
         return tuple(r[None] for r in results)
 
     in_specs = (grad_spec, row_spec, row_spec) * 3

time: 208 us -> 180 us (0.87)
  Pallas kernels: 197 us -> 179 us
  local copies, waits for them, and re-layouts: 10.5 us -> 0 us
    pallas_call x1 -> x2, Pallas kernels: 197 us -> 179 us  [the longest x1 176 us: step_local(): pl.pallas_call(body, out_shape=tuple(part_shape), in_specs=[anywhere] * 6...]
    unnamed x19 -> x0, local copies, waits for them, and re-layouts: 10.5 us -> none
where the time goes in v2:
time: 180 us
  Pallas kernels  179 us (99%)
    pallas_call x1, Pallas kernels, step_local(): pl.pallas_call(body, out_shape=tuple(part_shape), in_specs=[anywhere] * 6...  176 us

profile of v2, /device:TPU:21, one launch (start us, length us, event | category | flops | bytes accessed | tf_op | source)
XLA Modules:
  0.0 179.9 jit_solution(15736970740236392044)
XLA Ops:
  0.6 176.0 %muon.1 = (f32[96,1536]{1,0:T(8,128)}, bf16[96,1536]{1,0:T(8,128)(2,1)}, f32[96,512]{1,0:T(8,128)}, bf16[96,512]{1,0:T(8,128)(2,1)}, f32[32,1536]{1,0:T(8,128)}, /*index=5*/bf16[32,1536]{1,0:T(8,128)(2,1)}) custom-call(f32[1536,1536]{1,0:T(8,128)} %bitcast.18, f32[1536,512]{1,0:T(8,128)} %bitcast.19, f32[512,1536]{1,0:T(8,128)} %bitcast.20, ...), custom_call_target="tpu_custom_call" | custom-call | tf_op jit(solution)/shard_map/muon/pallas_call | solution.py:558
  176.6 3.2 %results.1 = (f32[96,1536]{1,0:T(8,128)}, f32[96,1536]{1,0:T(8,128)}, bf16[96,1536]{1,0:T(8,128)(2,1)}, f32[96,512]{1,0:T(8,128)}, f32[96,512]{1,0:T(8,128)}, /*...) custom-call(f32[96,1536]{1,0:T(8,128)} %get-tuple-element.24.refs_0_, ...), custom_call_target="tpu_custom_call" | custom-call | tf_op jit(solution)/shard_map/results/pallas_call | solution.py:572

commit v3 on v2

--- a/solution.py
+++ b/solution.py
@@ -127,70 +127,79 @@
 
 
 class Gather:
-    def __init__(self, place, full, rows, panels, rsend, rrecv, fsend, frecv):
-        self.pl, self.full, self.rows, self.panels = place, full, rows, panels
+    def __init__(self, place, full, other, rows, to, rsend, rrecv, fsend, frecv):
+        self.pl, self.full, self.other, self.rows, self.to = place, full, other, rows, to
         self.rsend, self.rrecv, self.fsend, self.frecv = rsend, rrecv, fsend, frecv
         self.half_rows = rows // 2
         self.n = place.chips
         self.pieces = self.n - 1
 
-    def base(self, chip, core):
-        return ((core * self.n + chip) if self.panels else (chip * 2 + core)) * self.rows
-
-    def piece(self, way, q, core, lag):
+    def rows_of(self, way, q, lag):
         hop = q // 2 + lag
-        chip = self.pl.at(-hop if way == 0 else hop)
+        slot = 0 if hop == 0 else min(2 * hop - 1 + way, self.n - 1)
         half = way if q % 2 == 0 else 1 - way
-        row = self.base(chip, core) + half * self.half_rows
-        return self.full.at[ds(row, self.half_rows, 16), :]
+        return pl.ds(slot * self.rows + half * self.half_rows, self.half_rows)
 
     def ring_copy(self, way, q):
-        ref = self.piece(way, q, self.pl.core, 0)
-        return remote(ref, ref, self.rsend.at[way, q], self.rrecv.at[way, q], self.pl.next(way))
-
-    def arrival(self, way, q):
-        ref = self.piece(way, q, self.pl.core, 1)
-        return remote(ref, ref, self.rsend.at[way, q], self.rrecv.at[way, q], self.pl.next(way))
-
-    def forward(self, way, q, core):
-        ref = self.piece(way, q, core, 1)
-        return remote(ref, ref, self.fsend.at[way, q], self.frecv.at[way, q], self.pl.partner)
-
-    def own_rows(self, core):
-        return self.full.at[ds(self.base(self.pl.chip, core), self.rows, 32), :]
-
-    def forward_own(self, core):
-        ref = self.own_rows(core)
-        return remote(ref, ref, self.fsend.at[0, self.pieces], self.frecv.at[0, self.pieces], self.pl.partner)
+        return remote(self.full.at[self.rows_of(way, q, 0), :], self.full.at[self.rows_of(way, q, 1), :],
+                      self.rsend.at[way, q], self.rrecv.at[way, q], self.pl.next(way))
+
+    def forward(self, way, q):
+        rows = self.rows_of(way, q, 1)
+        return remote(self.full.at[rows, :], self.other.at[rows, :], self.fsend.at[way, q], self.frecv.at[way, q], self.pl.partner)
+
+    def forward_own(self):
+        rows = pl.ds(0, self.rows)
+        return remote(self.full.at[rows, :], self.other.at[rows, :], self.fsend.at[0, self.pieces], self.frecv.at[0, self.pieces], self.pl.partner)
+
+    def sending(self, fn):
+        if self.to is None:
+            fn()
+        else:
+            pl.when(self.pl.core != self.to)(fn)
 
     def step(self, q):
         if q == 0:
             for k in (0, 1):
                 for way in (0, 1):
                     self.ring_copy(way, k).start()
-            self.forward_own(self.pl.core).start()
+            self.sending(lambda: self.forward_own().start())
         else:
             for way in (0, 1):
-                self.arrival(way, q - 1).wait_recv()
+                self.ring_copy(way, q - 1).wait_recv()
                 if q + 1 < self.pieces:
                     self.ring_copy(way, q + 1).start()
-                self.forward(way, q - 1, self.pl.core).start()
+
+            def hand_on():
+                for way in (0, 1):
+                    self.forward(way, q - 1).start()
+            self.sending(hand_on)
 
     def steps(self):
         return self.pieces + 1
 
     def finish(self):
-        self.forward_own(1 - self.pl.core).wait_recv()
+        def run():
+            self.forward_own().wait_recv()
+            for way in (0, 1):
+                for q in range(self.pieces):
+                    self.forward(way, q).wait_recv()
+        if self.to is None:
+            run()
+        else:
+            pl.when(self.pl.core == self.to)(run)
+
+    def drain(self):
         for way in (0, 1):
             for q in range(self.pieces):
-                self.forward(way, q, 1 - self.pl.core).wait_recv()
-
-    def drain(self):
-        self.forward_own(self.pl.core).wait_send()
-        for way in (0, 1):
-            for q in range(self.pieces):
-                self.forward(way, q, self.pl.core).wait_send()
                 self.ring_copy(way, q).wait_send()
+
+        def run():
+            self.forward_own().wait_send()
+            for way in (0, 1):
+                for q in range(self.pieces):
+                    self.forward(way, q).wait_send()
+        self.sending(run)
 
 
 def squares(mat):
@@ -225,8 +234,13 @@
 
     scat = [Scatter(place, grads[k], sc['own'][k], sc['pair'][k], sc['ring'][k], sc['load'].at[k], sc['psend'].at[k], sc['precv'].at[k],
                     sc['rsend'].at[k], sc['rrecv'].at[k]) for k in range(3)]
-    fulls = [sc['x'][0], sc['tall'], sc['xd']]
-    gath = [Gather(place, fulls[k], sc['own'][k].shape[1], k == 0, sc['gsend'].at[k], sc['grecv'].at[k], sc['fsend'].at[k], sc['frecv'].at[k]) for k in range(3)]
+    xo, xp = sc['xo'], sc['xp']
+    xd, tall = sc['xd'], sc['tall']
+    small, wide = xd.shape
+    fulls = [xo[0], tall.at[pl.ds(0, wide // 2), :], xd.at[pl.ds(0, small // 2), :]]
+    others = [xp[0], tall.at[pl.ds(wide // 2, wide // 2), :], xd.at[pl.ds(small // 2, small // 2), :]]
+    gath = [Gather(place, fulls[k], others[k], sc['own'][k].shape[1], (None, 0, 1)[k], sc['gsend'].at[k], sc['grecv'].at[k], sc['fsend'].at[k], sc['frecv'].at[k])
+            for k in range(3)]
 
     scat[0].start()
     in_copies = []
@@ -265,7 +279,7 @@
 
     def write_x(k, norm):
         rows = sc['own'][k].shape[1]
-        fulls[k][ds(gath[k].base(chip, core), rows, 32), :] = (sc['mom'][k][...] / norm).astype(BF16)
+        fulls[k][0:rows, :] = (sc['mom'][k][...] / norm).astype(BF16)
 
     for q in range(pieces):
         scat[0].step(q)
@@ -304,54 +318,71 @@
         return run
 
     background(0, 0, both(scat, 3))
-    for q, place_at in ((4, (0, 3)), (5, (0, 5)), (6, (1, 1))):
+    for q, place_at in ((4, (0, 4)), (5, (0, 7)), (6, (1, 2))):
         background(*place_at, both(scat, q))
-    background(1, 5, ud_momentum)
-    background(2, 2, ud_write)
-    times = ((2, 2), (2, 5), (2, 6), (3, 1), (3, 2), (3, 3), (3, 5), (3, 6))
+    background(1, 7, ud_momentum)
+    background(2, 4, ud_write)
+    times = ((2, 4), (2, 7), (3, 1), (3, 3), (3, 5), (3, 6), (4, 0), (4, 2))
     for q in range(gath[1].steps()):
         background(*times[q], both(gath, q))
 
-    xs, a, b, qacc = sc['x'], sc['a'], sc['b'], sc['qacc']
-    size = a.shape[0]
-    half = size // 2
+    aoo, aop, app, ar = sc['aoo'], sc['aop'], sc['app'], sc['ar']
+    bo, bp = sc['bo'], sc['bp']
+    half, size = xo[0].shape
     third = size // 3
-    mine = ds(core * half, half, 128)
-    theirs = ds((1 - core) * half, half, 128)
-
-    def a_copy(i):
-        if i == 0:
-            return remote(a.at[mine, mine], a.at[mine, mine], sc['asend'].at[0], sc['arecv'].at[0], place.partner)
-        rows = ds(core * half + (i - 1) * (half // 2), half // 2, 128)
-        return remote(a.at[rows, theirs], a.at[rows, theirs], sc['asend'].at[i], sc['arecv'].at[i], place.partner)
-
-    def x_copy(x, n):
-        ref = x.at[mine, pl.ds(n * third, third)]
-        return remote(ref, ref, sc['xsend'].at[n], sc['xrecv'].at[n], place.partner)
-
-    def x_wait(x):
+    parts = 3
+    blk = half // parts
+
+    def rows_at(i):
+        return pl.ds(i * blk, blk)
+
+    def cross_copy(t):
+        return remote(aop.at[rows_at(t), rows_at((t + 1) % parts)], ar.at[t], sc['asend'].at[t], sc['arecv'].at[t], place.partner)
+
+    def own_copy():
+        return remote(aoo, app, sc['asend'].at[parts], sc['arecv'].at[parts], place.partner)
+
+    def x_copy(way, n):
+        cols = pl.ds(n * third, third)
+        return remote(xo[way].at[:, cols], xp[way].at[:, cols], sc['xsend'].at[n], sc['xrecv'].at[n], place.partner)
+
+    def x_wait(way):
         for n in range(3):
-            x_copy(x, n).wait_recv()
-            x_copy(x, n).wait_send()
-
-    def grams(x, slot, wait):
+            x_copy(way, n).wait_recv()
+            x_copy(way, n).wait_send()
+
+    def mirror(ref):
+        for i in range(parts):
+            for j in range(i + 1, parts):
+                ref[rows_at(j), rows_at(i)] = ref[rows_at(i), rows_at(j)].T
+
+    def grams(way, slot, wait):
+        x, y = xo[way], xp[way]
         slot(0)
-        a[mine, mine] = dot_nt(x[mine, :], x[mine, :]).astype(BF16)
+        for i in range(parts):
+            aoo[rows_at(i), i * blk:] = dot_nt(x[rows_at(i), :], x[i * blk:, :]).astype(BF16)
+        slot(1)
         wait()
-        slot(1)
-        a_copy(0).start()
-        for i in (0, 1):
-            rows = ds(core * half + i * (half // 2), half // 2, 128)
-            a[rows, theirs] = dot_nt(x[rows, :], x[theirs, :]).astype(BF16)
-            a_copy(1 + i).start()
-
-    def a_wait():
-        for i in range(3):
-            a_copy(i).wait_recv()
+        for t in range(parts):
+            u = (t + 1) % parts
+            aop[rows_at(t), rows_at(u)] = dot_nt(x[rows_at(t), :], y[rows_at(u), :]).astype(BF16)
+        for t in range(parts):
+            cross_copy(t).start()
+        slot(2)
+        for t in range(parts):
+            aop[rows_at(t), rows_at(t)] = dot_nt(x[rows_at(t), :], y[rows_at(t), :]).astype(BF16)
+        mirror(aoo)
+        own_copy().start()
+        slot(3)
+        for t in range(parts):
+            cross_copy(t).wait_recv()
+        for t in range(parts):
+            aop[rows_at((t + 1) % parts), rows_at(t)] = ar[t].T
 
     def a_drain():
-        for i in range(3):
-            a_copy(i).wait_send()
+        for t in range(parts):
+            cross_copy(t).wait_send()
+        own_copy().wait_send()
 
     def poly(lin, acc):
         return (COEF_B * lin.astype(F32) + COEF_C * acc.astype(BF16).astype(F32)).astype(BF16)
@@ -360,11 +391,11 @@
         return (COEF_A * old.astype(F32) + upd.astype(BF16).astype(F32)).astype(BF16)
 
     def ns_step(pair, parity):
-        x, xn = xs[parity], xs[1 - parity]
+        x, y, xn = xo[parity], xp[parity], xo[1 - parity]
 
         def slot(s):
             for (t, u), fns in tasks.items():
-                if u == s and t % 2 == parity:
+                if u == s and t % 2 == parity and t < NS_STEPS - 1:
                     def run(fns=fns):
                         for fn in fns:
                             fn()
@@ -379,28 +410,24 @@
 
                 @pl.when(pair > 0)
                 def _():
-                    x_wait(x)
+                    x_wait(0)
             else:
-                x_wait(x)
-
-        grams(x, slot, wait)
-        slot(2)
-        for n in (0, 1):
-            cols = pl.ds(n * half, half)
-            qacc[:, cols] = dot_nn(a[mine, mine], a[mine, cols])
-        slot(3)
-        a_wait()
-        for n in (0, 1):
-            cols = pl.ds(n * half, half)
-            b[:, cols] = poly(a[mine, cols], qacc[:, cols] + dot_nn(a[mine, theirs], a[theirs, cols]))
+                x_wait(1)
+
+        grams(parity, slot, wait)
+        for i in range(parts):
+            sq = dot_nt(aoo[rows_at(i), :], aoo[i * blk:, :]) + dot_nt(aop[rows_at(i), :], aop[i * blk:, :])
+            bo[rows_at(i), i * blk:] = poly(aoo[rows_at(i), i * blk:], sq)
         slot(4)
+        own_copy().wait_recv()
+        bp[...] = poly(aop[...], dot_nn(aoo[...], aop[...]) + dot_nn(aop[...], app[...]))
+        mirror(bo)
         a_drain()
         for n in range(3):
+            slot(5 + n)
             cols = pl.ds(n * third, third)
-            xn[mine, cols] = renew(x[mine, cols], dot_nn(b[...], x[:, cols]))
-            x_copy(xn, n).start()
-            if n < 2:
-                slot(5 + n)
+            xn[:, cols] = renew(x[:, cols], dot_nn(bo[...], x[:, cols]) + dot_nn(bp[...], y[:, cols]))
+            x_copy(1 - parity, n).start()
 
     def ns_pair(pair, carry):
         ns_step(pair, 0)
@@ -409,23 +436,23 @@
 
     lax.fori_loop(0, NS_STEPS // 2, ns_pair, 0)
 
-    x = xs[0]
-    grams(x, lambda s: None, lambda: x_wait(x))
-    a_wait()
-    rows_local = sc['own'][0].shape[1]
-    own_rows = ds(core * half + chip * rows_local, rows_local, 32)
-    for n in (0, 1):
-        cols = pl.ds(n * half, half)
-        b[0:rows_local, cols] = poly(a[own_rows, cols], dot_nn(a[own_rows, :], a[:, cols]))
+    def last_slot(s):
+        for fn in tasks.get((NS_STEPS - 1, s), []):
+            fn()
+
+    grams(0, last_slot, lambda: x_wait(0))
+    own_copy().wait_recv()
+    top = pl.ds(0, sc['own'][0].shape[1])
+    bo[top, :] = poly(aoo[top, :], dot_nt(aoo[top, :], aoo[...]) + dot_nt(aop[top, :], aop[...]))
+    bp[top, :] = poly(aop[top, :], dot_nn(aoo[top, :], aop[...]) + dot_nn(aop[top, :], app[...]))
     a_drain()
-    sc['oa'][...] = renew(x[own_rows, :], dot_nn(b[0:rows_local, :], x[...]))
+    sc['oa'][...] = renew(xo[0][top, :], dot_nn(bo[top, :], xo[0][...]) + dot_nn(bp[top, :], xp[0][...]))
     out_copy(0, 1, sc['oa']).start()
 
     for k in (1, 2):
         gath[k].finish()
         gath[k].drain()
-    xd, tall, bu = sc['xd'], sc['tall'], sc['bu']
-    small, wide = xd.shape
+    bu = sc['bu']
     up_rows, down_rows = sc['own'][1].shape[1], sc['own'][2].shape[1]
     up_send, down_send = sc['up_send'], sc['down_send']
     up_copy = remote(up_send, sc['ou'], sc['osend'].at[0], sc['orecv'].at[0], place.partner)
@@ -444,10 +471,10 @@
         lax.fori_loop(0, NS_STEPS - 1, step, 0)
         bu[0] = dot_tn(tall[...], tall[...]).astype(BF16)
         bu[1] = poly(bu[0], dot_nn(bu[0], bu[0]))
-        other = tall[ds((chip * 2 + 1) * up_rows, up_rows, 32), :]
+        other = tall[half_wide:half_wide + up_rows, :]
         up_send[...] = renew(other, dot_nn(other, bu[1]))
         up_copy.start()
-        own = tall[ds(chip * 2 * up_rows, up_rows, 32), :]
+        own = tall[0:up_rows, :]
         sc['ou'][...] = renew(own, dot_nn(own, bu[1]))
         out_copy(1, 1, sc['ou']).start()
         down_copy.wait_recv()
@@ -467,12 +494,12 @@
         bu[0] = dot_nt(xd[...], xd[...]).astype(BF16)
 
         def rows_of(which):
-            rows = ds((chip * 2 + which) * down_rows, down_rows, 32)
+            rows = pl.ds(which * (small // 2), down_rows)
             part = poly(bu[0, rows, :], dot_nn(bu[0, rows, :], bu[0]))
             return renew(xd[rows, :], dot_nn(part, xd[...]))
-        down_send[...] = rows_of(0)
+        down_send[...] = rows_of(1)
         down_copy.start()
-        sc['od'][...] = rows_of(1)
+        sc['od'][...] = rows_of(0)
         out_copy(2, 1, sc['od']).start()
         up_copy.wait_recv()
         out_copy(1, 1, sc['ou']).start()
@@ -524,11 +551,13 @@
             add(('pair', k), pltpu.VMEM((chips, rows, cols), F32))
             add(('ring', k), pltpu.VMEM((2, chips // 2, rows, cols), F32))
             add(('mom', k), pltpu.VMEM((rows, cols), F32))
-        add(('x', 0), pltpu.VMEM((size, size), BF16))
-        add(('x', 1), pltpu.VMEM((size, size), BF16))
-        add('a', pltpu.VMEM((size, size), BF16))
-        add('b', pltpu.VMEM((size // 2, size), BF16))
-        add('qacc', pltpu.VMEM((size // 2, size), F32))
+        half = size // 2
+        for name in ('xo', 'xp'):
+            add((name, 0), pltpu.VMEM((half, size), BF16))
+            add((name, 1), pltpu.VMEM((half, size), BF16))
+        for name in ('aoo', 'aop', 'app', 'bo', 'bp'):
+            add(name, pltpu.VMEM((half, half), BF16))
+        add('ar', pltpu.VMEM((3, half // 3, half // 3), BF16))
         add('tall', pltpu.VMEM((wide, small), BF16))
         add('xd', pltpu.VMEM((small, wide), BF16))
         add('bu', pltpu.VMEM((2, small, small), BF16))
@@ -538,7 +567,7 @@
         add(('norm', 1), pltpu.VMEM((group, 16, 128), F32))
         for name, shape in (('load', (3, chips)), ('psend', (3, chips)), ('precv', (3, chips)), ('rsend', (3, 2, pieces)), ('rrecv', (3, 2, pieces)),
                             ('gsend', (3, 2, pieces)), ('grecv', (3, 2, pieces)), ('fsend', (3, 2, chips)), ('frecv', (3, 2, chips)),
-                            ('nsend', (2, group)), ('nrecv', (2, group)), ('insem', (3,)), ('outsem', (6,)), ('asend', (3,)), ('arecv', (3,)),
+                            ('nsend', (2, group)), ('nrecv', (2, group)), ('insem', (3,)), ('outsem', (6,)), ('asend', (4,)), ('arecv', (4,)),
                             ('xsend', (3,)), ('xrecv', (3,)), ('osend', (2,)), ('orecv', (2,))):
             add(name, dma(shape))
 

time: 180 us -> 190 us (1.056)
  Pallas kernels: 179 us -> 189 us
    pallas_call x1, Pallas kernels: 176 us -> 186 us  [step_local(): pl.pallas_call(body, out_shape=tuple(part_shape), in_specs=[anywhere] * 6...]
where the time goes in v3:
time: 190 us
  Pallas kernels  189 us (99%)
    pallas_call x1, Pallas kernels, step_local(): pl.pallas_call(body, out_shape=tuple(part_shape), in_specs=[anywhere] * 6...  186 us

profile of v3, /device:TPU:21, one launch (start us, length us, event | category | flops | bytes accessed | tf_op | source)
XLA Modules:
  0.0 190.1 jit_solution(7741437854537274665)
XLA Ops:
  0.6 186.2 %muon.1 = (f32[96,1536]{1,0:T(8,128)}, bf16[96,1536]{1,0:T(8,128)(2,1)}, f32[96,512]{1,0:T(8,128)}, bf16[96,512]{1,0:T(8,128)(2,1)}, f32[32,1536]{1,0:T(8,128)}, /*index=5*/bf16[32,1536]{1,0:T(8,128)(2,1)}) custom-call(f32[1536,1536]{1,0:T(8,128)} %bitcast.18, f32[1536,512]{1,0:T(8,128)} %bitcast.19, f32[512,1536]{1,0:T(8,128)} %bitcast.20, ...), custom_call_target="tpu_custom_call" | custom-call | tf_op jit(solution)/shard_map/muon/pallas_call | solution.py:587
  186.9 3.2 %results.1 = (f32[96,1536]{1,0:T(8,128)}, f32[96,1536]{1,0:T(8,128)}, bf16[96,1536]{1,0:T(8,128)(2,1)}, f32[96,512]{1,0:T(8,128)}, f32[96,512]{1,0:T(8,128)}, /*...) custom-call(f32[96,1536]{1,0:T(8,128)} %get-tuple-element.24.refs_0_, ...), custom_call_target="tpu_custom_call" | custom-call | tf_op jit(solution)/shard_map/results/pallas_call | solution.py:601

commit v4 on v3

--- a/solution.py
+++ b/solution.py
@@ -234,11 +234,13 @@
 
     scat = [Scatter(place, grads[k], sc['own'][k], sc['pair'][k], sc['ring'][k], sc['load'].at[k], sc['psend'].at[k], sc['precv'].at[k],
                     sc['rsend'].at[k], sc['rrecv'].at[k]) for k in range(3)]
-    xo, xp = sc['xo'], sc['xp']
+    xs = sc['x']
+    size = xs[0].shape[0]
+    half = size // 2
     xd, tall = sc['xd'], sc['tall']
     small, wide = xd.shape
-    fulls = [xo[0], tall.at[pl.ds(0, wide // 2), :], xd.at[pl.ds(0, small // 2), :]]
-    others = [xp[0], tall.at[pl.ds(wide // 2, wide // 2), :], xd.at[pl.ds(small // 2, small // 2), :]]
+    fulls = [xs[0].at[pl.ds(0, half), :], tall.at[pl.ds(0, wide // 2), :], xd.at[pl.ds(0, small // 2), :]]
+    others = [xs[0].at[pl.ds(half, half), :], tall.at[pl.ds(wide // 2, wide // 2), :], xd.at[pl.ds(small // 2, small // 2), :]]
     gath = [Gather(place, fulls[k], others[k], sc['own'][k].shape[1], (None, 0, 1)[k], sc['gsend'].at[k], sc['grecv'].at[k], sc['fsend'].at[k], sc['frecv'].at[k])
             for k in range(3)]
 
@@ -318,71 +320,78 @@
         return run
 
     background(0, 0, both(scat, 3))
-    for q, place_at in ((4, (0, 4)), (5, (0, 7)), (6, (1, 2))):
+    for q, place_at in ((4, (0, 3)), (5, (0, 8)), (6, (1, 2))):
         background(*place_at, both(scat, q))
-    background(1, 7, ud_momentum)
-    background(2, 4, ud_write)
-    times = ((2, 4), (2, 7), (3, 1), (3, 3), (3, 5), (3, 6), (4, 0), (4, 2))
+    background(2, 1, ud_momentum)
+    background(2, 6, ud_write)
+    times = ((2, 6), (3, 2), (3, 3), (3, 5), (3, 9), (4, 1), (4, 3), (4, 4))
     for q in range(gath[1].steps()):
         background(*times[q], both(gath, q))
 
-    aoo, aop, app, ar = sc['aoo'], sc['aop'], sc['app'], sc['ar']
-    bo, bp = sc['bo'], sc['bp']
-    half, size = xo[0].shape
-    third = size // 3
+    grids, b, ar, qacc = sc['a'], sc['b'], sc['ar'], sc['qacc']
     parts = 3
     blk = half // parts
+    tiles = tuple((n * blk, blk) for n in range(2 * parts))
 
     def rows_at(i):
         return pl.ds(i * blk, blk)
 
-    def cross_copy(t):
-        return remote(aop.at[rows_at(t), rows_at((t + 1) % parts)], ar.at[t], sc['asend'].at[t], sc['arecv'].at[t], place.partner)
-
-    def own_copy():
-        return remote(aoo, app, sc['asend'].at[parts], sc['arecv'].at[parts], place.partner)
+    def far_at(i):
+        return pl.ds(half + i * blk, blk)
+
+    def cross_copy(way, t):
+        return remote(grids[way].at[rows_at(t), far_at((t + 1) % parts)], ar.at[t], sc['asend'].at[way, t], sc['arecv'].at[way, t], place.partner)
+
+    def own_copy(way, i):
+        width = half - i * blk
+        return remote(grids[way].at[rows_at(i), pl.ds(i * blk, width)], grids[way].at[far_at(i), pl.ds(half + i * blk, width)],
+                      sc['asend'].at[way, parts + i], sc['arecv'].at[way, parts + i], place.partner)
 
     def x_copy(way, n):
-        cols = pl.ds(n * third, third)
-        return remote(xo[way].at[:, cols], xp[way].at[:, cols], sc['xsend'].at[n], sc['xrecv'].at[n], place.partner)
+        cols = pl.ds(*tiles[n])
+        return remote(xs[way].at[pl.ds(0, half), cols], xs[way].at[pl.ds(half, half), cols], sc['xsend'].at[n], sc['xrecv'].at[n], place.partner)
 
     def x_wait(way):
-        for n in range(3):
+        for n in range(len(tiles)):
             x_copy(way, n).wait_recv()
             x_copy(way, n).wait_send()
 
-    def mirror(ref):
+    def mirror(ref, at):
         for i in range(parts):
             for j in range(i + 1, parts):
-                ref[rows_at(j), rows_at(i)] = ref[rows_at(i), rows_at(j)].T
+                ref[at(j), at(i)] = ref[at(i), at(j)].T
 
     def grams(way, slot, wait):
-        x, y = xo[way], xp[way]
+        x, a = xs[way], grids[way]
         slot(0)
         for i in range(parts):
-            aoo[rows_at(i), i * blk:] = dot_nt(x[rows_at(i), :], x[i * blk:, :]).astype(BF16)
+            a[rows_at(i), i * blk:half] = dot_nt(x[rows_at(i), :], x[i * blk:half, :]).astype(BF16)
+        for i in range(parts):
+            own_copy(way, i).start()
         slot(1)
         wait()
         for t in range(parts):
-            u = (t + 1) % parts
-            aop[rows_at(t), rows_at(u)] = dot_nt(x[rows_at(t), :], y[rows_at(u), :]).astype(BF16)
+            a[rows_at(t), far_at((t + 1) % parts)] = dot_nt(x[rows_at(t), :], x[far_at((t + 1) % parts), :]).astype(BF16)
         for t in range(parts):
-            cross_copy(t).start()
+            cross_copy(way, t).start()
         slot(2)
+        mirror(a, rows_at)
         for t in range(parts):
-            aop[rows_at(t), rows_at(t)] = dot_nt(x[rows_at(t), :], y[rows_at(t), :]).astype(BF16)
-        mirror(aoo)
-        own_copy().start()
-        slot(3)
+            a[rows_at(t), far_at(t)] = dot_nt(x[rows_at(t), :], x[far_at(t), :]).astype(BF16)
+
+    def crosses(way):
+        a = grids[way]
         for t in range(parts):
-            cross_copy(t).wait_recv()
+            own_copy(way, t).wait_recv()
+            cross_copy(way, t).wait_recv()
         for t in range(parts):
-            aop[rows_at((t + 1) % parts), rows_at(t)] = ar[t].T
-
-    def a_drain():
+            a[rows_at((t + 1) % parts), far_at(t)] = ar[t].T
+        mirror(a, far_at)
+
+    def a_drain(way):
         for t in range(parts):
-            cross_copy(t).wait_send()
-        own_copy().wait_send()
+            own_copy(way, t).wait_send()
+            cross_copy(way, t).wait_send()
 
     def poly(lin, acc):
         return (COEF_B * lin.astype(F32) + COEF_C * acc.astype(BF16).astype(F32)).astype(BF16)
@@ -391,7 +400,7 @@
         return (COEF_A * old.astype(F32) + upd.astype(BF16).astype(F32)).astype(BF16)
 
     def ns_step(pair, parity):
-        x, y, xn = xo[parity], xp[parity], xo[1 - parity]
+        x, xn, a = xs[parity], xs[1 - parity], grids[parity]
 
         def slot(s):
             for (t, u), fns in tasks.items():
@@ -416,17 +425,20 @@
 
         grams(parity, slot, wait)
         for i in range(parts):
-            sq = dot_nt(aoo[rows_at(i), :], aoo[i * blk:, :]) + dot_nt(aop[rows_at(i), :], aop[i * blk:, :])
-            bo[rows_at(i), i * blk:] = poly(aoo[rows_at(i), i * blk:], sq)
+            qacc[rows_at(i), i * blk:] = dot_nt(a[rows_at(i), 0:half], a[i * blk:half, 0:half])
+        slot(3)
+        crosses(parity)
+        for i in range(parts):
+            sq = qacc[rows_at(i), i * blk:] + dot_nt(a[rows_at(i), half:], a[i * blk:half, half:])
+            b[rows_at(i), i * blk:half] = poly(a[rows_at(i), i * blk:half], sq)
         slot(4)
-        own_copy().wait_recv()
-        bp[...] = poly(aop[...], dot_nn(aoo[...], aop[...]) + dot_nn(aop[...], app[...]))
-        mirror(bo)
-        a_drain()
-        for n in range(3):
+        b[:, half:] = poly(a[0:half, half:], dot_nn(a[0:half, :], a[:, half:]))
+        mirror(b, rows_at)
+        a_drain(parity)
+        for n, (left, width) in enumerate(tiles):
             slot(5 + n)
-            cols = pl.ds(n * third, third)
-            xn[:, cols] = renew(x[:, cols], dot_nn(bo[...], x[:, cols]) + dot_nn(bp[...], y[:, cols]))
+            cols = pl.ds(left, width)
+            xn[0:half, cols] = renew(x[0:half, cols], dot_nn(b[...], x[:, cols]))
             x_copy(1 - parity, n).start()
 
     def ns_pair(pair, carry):
@@ -441,13 +453,16 @@
             fn()
 
     grams(0, last_slot, lambda: x_wait(0))
-    own_copy().wait_recv()
+    last_slot(3)
+    crosses(0)
+    a = grids[0]
     top = pl.ds(0, sc['own'][0].shape[1])
-    bo[top, :] = poly(aoo[top, :], dot_nt(aoo[top, :], aoo[...]) + dot_nt(aop[top, :], aop[...]))
-    bp[top, :] = poly(aop[top, :], dot_nn(aoo[top, :], aop[...]) + dot_nn(aop[top, :], app[...]))
-    a_drain()
-    sc['oa'][...] = renew(xo[0][top, :], dot_nn(bo[top, :], xo[0][...]) + dot_nn(bp[top, :], xp[0][...]))
+    b[top, 0:half] = poly(a[top, 0:half], dot_nt(a[top, :], a[0:half, :]))
+    b[top, half:] = poly(a[top, half:], dot_nn(a[top, :], a[:, half:]))
+    a_drain(0)
+    sc['oa'][...] = renew(xs[0][top, :], dot_nn(b[top, :], xs[0][...]))
     out_copy(0, 1, sc['oa']).start()
+    last_slot(4)
 
     for k in (1, 2):
         gath[k].finish()
@@ -552,11 +567,12 @@
             add(('ring', k), pltpu.VMEM((2, chips // 2, rows, cols), F32))
             add(('mom', k), pltpu.VMEM((rows, cols), F32))
         half = size // 2
-        for name in ('xo', 'xp'):
-            add((name, 0), pltpu.VMEM((half, size), BF16))
-            add((name, 1), pltpu.VMEM((half, size), BF16))
-        for name in ('aoo', 'aop', 'app', 'bo', 'bp'):
-            add(name, pltpu.VMEM((half, half), BF16))
+        add(('x', 0), pltpu.VMEM((size, size), BF16))
+        add(('x', 1), pltpu.VMEM((size, size), BF16))
+        add(('a', 0), pltpu.VMEM((size, size), BF16))
+        add(('a', 1), pltpu.VMEM((size, size), BF16))
+        add('qacc', pltpu.VMEM((half, half), F32))
+        add('b', pltpu.VMEM((half, size), BF16))
         add('ar', pltpu.VMEM((3, half // 3, half // 3), BF16))
         add('tall', pltpu.VMEM((wide, small), BF16))
         add('xd', pltpu.VMEM((small, wide), BF16))
@@ -567,8 +583,8 @@
         add(('norm', 1), pltpu.VMEM((group, 16, 128), F32))
         for name, shape in (('load', (3, chips)), ('psend', (3, chips)), ('precv', (3, chips)), ('rsend', (3, 2, pieces)), ('rrecv', (3, 2, pieces)),
                             ('gsend', (3, 2, pieces)), ('grecv', (3, 2, pieces)), ('fsend', (3, 2, chips)), ('frecv', (3, 2, chips)),
-                            ('nsend', (2, group)), ('nrecv', (2, group)), ('insem', (3,)), ('outsem', (6,)), ('asend', (4,)), ('arecv', (4,)),
-                            ('xsend', (3,)), ('xrecv', (3,)), ('osend', (2,)), ('orecv', (2,))):
+                            ('nsend', (2, group)), ('nrecv', (2, group)), ('insem', (3,)), ('outsem', (6,)), ('asend', (2, 6)), ('arecv', (2, 6)),
+                            ('xsend', (6,)), ('xrecv', (6,)), ('osend', (2,)), ('orecv', (2,))):
             add(name, dma(shape))
 
         def body(*refs):

time: 190 us -> 184 us (0.968)
  Pallas kernels: 189 us -> 184 us
    pallas_call x1, Pallas kernels: 186 us -> 180 us  [step_local(): pl.pallas_call(body, out_shape=tuple(part_shape), in_specs=[anywhere] * 6...]
where the time goes in v4:
time: 184 us
  Pallas kernels  184 us (100%)
    pallas_call x1, Pallas kernels, step_local(): pl.pallas_call(body, out_shape=tuple(part_shape), in_specs=[anywhere] * 6...  180 us

profile of v4, /device:TPU:21, one launch (start us, length us, event | category | flops | bytes accessed | tf_op | source)
XLA Modules:
  0.0 184.3 jit_solution(8846019187294384471)
XLA Ops:
  0.6 180.4 %muon.1 = (f32[96,1536]{1,0:T(8,128)}, bf16[96,1536]{1,0:T(8,128)(2,1)}, f32[96,512]{1,0:T(8,128)}, bf16[96,512]{1,0:T(8,128)(2,1)}, f32[32,1536]{1,0:T(8,128)}, /*index=5*/bf16[32,1536]{1,0:T(8,128)(2,1)}) custom-call(f32[1536,1536]{1,0:T(8,128)} %bitcast.18, f32[1536,512]{1,0:T(8,128)} %bitcast.19, f32[512,1536]{1,0:T(8,128)} %bitcast.20, ...), custom_call_target="tpu_custom_call" | custom-call | tf_op jit(solution)/shard_map/muon/pallas_call | solution.py:603
  181.0 3.2 %results.1 = (f32[96,1536]{1,0:T(8,128)}, f32[96,1536]{1,0:T(8,128)}, bf16[96,1536]{1,0:T(8,128)(2,1)}, f32[96,512]{1,0:T(8,128)}, f32[96,512]{1,0:T(8,128)}, /*...) custom-call(f32[96,1536]{1,0:T(8,128)} %get-tuple-element.24.refs_0_, ...), custom_call_target="tpu_custom_call" | custom-call | tf_op jit(solution)/shard_map/results/pallas_call | solution.py:617

commit v5 on v4

--- a/solution.py
+++ b/solution.py
@@ -320,18 +320,18 @@
         return run
 
     background(0, 0, both(scat, 3))
-    for q, place_at in ((4, (0, 3)), (5, (0, 8)), (6, (1, 2))):
+    for q, place_at in ((4, (0, 3)), (5, (0, 6)), (6, (1, 2))):
         background(*place_at, both(scat, q))
-    background(2, 1, ud_momentum)
-    background(2, 6, ud_write)
-    times = ((2, 6), (3, 2), (3, 3), (3, 5), (3, 9), (4, 1), (4, 3), (4, 4))
+    background(2, 0, ud_momentum)
+    background(2, 5, ud_write)
+    times = ((2, 5), (3, 1), (3, 3), (3, 5), (3, 6), (4, 1), (4, 3), (4, 4))
     for q in range(gath[1].steps()):
         background(*times[q], both(gath, q))
 
     grids, b, ar, qacc = sc['a'], sc['b'], sc['ar'], sc['qacc']
     parts = 3
     blk = half // parts
-    tiles = tuple((n * blk, blk) for n in range(2 * parts))
+    tiles = tuple((n * 2 * blk, 2 * blk) for n in range(parts))
 
     def rows_at(i):
         return pl.ds(i * blk, blk)
@@ -584,7 +584,7 @@
         for name, shape in (('load', (3, chips)), ('psend', (3, chips)), ('precv', (3, chips)), ('rsend', (3, 2, pieces)), ('rrecv', (3, 2, pieces)),
                             ('gsend', (3, 2, pieces)), ('grecv', (3, 2, pieces)), ('fsend', (3, 2, chips)), ('frecv', (3, 2, chips)),
                             ('nsend', (2, group)), ('nrecv', (2, group)), ('insem', (3,)), ('outsem', (6,)), ('asend', (2, 6)), ('arecv', (2, 6)),
-                            ('xsend', (6,)), ('xrecv', (6,)), ('osend', (2,)), ('orecv', (2,))):
+                            ('xsend', (3,)), ('xrecv', (3,)), ('osend', (2,)), ('orecv', (2,))):
             add(name, dma(shape))
 
         def body(*refs):

time: 184 us -> 168 us (0.913)
  Pallas kernels: 184 us -> 167 us
    pallas_call x1, Pallas kernels: 180 us -> 164 us  [step_local(): pl.pallas_call(body, out_shape=tuple(part_shape), in_specs=[anywhere] * 6...]
where the time goes in v5:
time: 168 us
  Pallas kernels  167 us (99%)
    pallas_call x1, Pallas kernels, step_local(): pl.pallas_call(body, out_shape=tuple(part_shape), in_specs=[anywhere] * 6...  164 us

profile of v5, /device:TPU:21, one launch (start us, length us, event | category | flops | bytes accessed | tf_op | source)
XLA Modules:
  0.0 168.1 jit_solution(17111043296006316044)
XLA Ops:
  0.6 164.2 %muon.1 = (f32[96,1536]{1,0:T(8,128)}, bf16[96,1536]{1,0:T(8,128)(2,1)}, f32[96,512]{1,0:T(8,128)}, bf16[96,512]{1,0:T(8,128)(2,1)}, f32[32,1536]{1,0:T(8,128)}, /*index=5*/bf16[32,1536]{1,0:T(8,128)(2,1)}) custom-call(f32[1536,1536]{1,0:T(8,128)} %bitcast.18, f32[1536,512]{1,0:T(8,128)} %bitcast.19, f32[512,1536]{1,0:T(8,128)} %bitcast.20, ...), custom_call_target="tpu_custom_call" | custom-call | tf_op jit(solution)/shard_map/muon/pallas_call | solution.py:603
  164.8 3.2 %results.1 = (f32[96,1536]{1,0:T(8,128)}, f32[96,1536]{1,0:T(8,128)}, bf16[96,1536]{1,0:T(8,128)(2,1)}, f32[96,512]{1,0:T(8,128)}, f32[96,512]{1,0:T(8,128)}, /*...) custom-call(f32[96,1536]{1,0:T(8,128)} %get-tuple-element.24.refs_0_, ...), custom_call_target="tpu_custom_call" | custom-call | tf_op jit(solution)/shard_map/results/pallas_call | solution.py:617

commit v6 on v5

--- a/solution.py
+++ b/solution.py
@@ -322,9 +322,9 @@
     background(0, 0, both(scat, 3))
     for q, place_at in ((4, (0, 3)), (5, (0, 6)), (6, (1, 2))):
         background(*place_at, both(scat, q))
-    background(2, 0, ud_momentum)
-    background(2, 5, ud_write)
-    times = ((2, 5), (3, 1), (3, 3), (3, 5), (3, 6), (4, 1), (4, 3), (4, 4))
+    background(1, 7, ud_momentum)
+    background(2, 4, ud_write)
+    times = ((2, 4), (2, 7), (3, 1), (3, 3), (3, 5), (3, 7), (4, 1), (4, 3))
     for q in range(gath[1].steps()):
         background(*times[q], both(gath, q))
 

time: 168 us -> 169 us (level)
  no operation moved by 1% of the time
where the time goes in v6:
time: 169 us
  Pallas kernels  168 us (99%)
    pallas_call x1, Pallas kernels, step_local(): pl.pallas_call(body, out_shape=tuple(part_shape), in_specs=[anywhere] * 6...  165 us

profile of v6, /device:TPU:21, one launch (start us, length us, event | category | flops | bytes accessed | tf_op | source)
XLA Modules:
  0.0 169.1 jit_solution(1875394428361177798)
XLA Ops:
  0.6 165.2 %muon.1 = (f32[96,1536]{1,0:T(8,128)}, bf16[96,1536]{1,0:T(8,128)(2,1)}, f32[96,512]{1,0:T(8,128)}, bf16[96,512]{1,0:T(8,128)(2,1)}, f32[32,1536]{1,0:T(8,128)}, /*index=5*/bf16[32,1536]{1,0:T(8,128)(2,1)}) custom-call(f32[1536,1536]{1,0:T(8,128)} %bitcast.18, f32[1536,512]{1,0:T(8,128)} %bitcast.19, f32[512,1536]{1,0:T(8,128)} %bitcast.20, ...), custom_call_target="tpu_custom_call" | custom-call | tf_op jit(solution)/shard_map/muon/pallas_call | solution.py:603
  165.8 3.2 %results.1 = (f32[96,1536]{1,0:T(8,128)}, f32[96,1536]{1,0:T(8,128)}, bf16[96,1536]{1,0:T(8,128)(2,1)}, f32[96,512]{1,0:T(8,128)}, f32[96,512]{1,0:T(8,128)}, /*...) custom-call(f32[96,1536]{1,0:T(8,128)} %get-tuple-element.24.refs_0_, ...), custom_call_target="tpu_custom_call" | custom-call | tf_op jit(solution)/shard_map/results/pallas_call | solution.py:617
